TPU v7x, 256 devices: a whole 4x4x8 slice. The times are simulated.
256 devices in a mesh: gx: 8 (over y, x_hi), gy: 4 (over x_lo, core), gz: 8 (over z).
Axes of the slice: x: 4 (x_hi: 2, x_lo: 2; x = x_hi * 2 + x_lo), y: 4, z: 8, core: 2. Of those that a mesh axis runs over, the one named last changes fastest.
Arguments:
- coeffs: bfloat16 [8, 4, 8, 128, 3200], P('gx', 'gy', 'gz'), may hold values from -6 to 6
- halo_rows: int32 [8, 4, 8, 32], P('gx', 'gy', 'gz'), may hold values from 0 to 127
- edge_source: int32 [8, 4, 8, 4, 128], P('gx', 'gy', 'gz'), may hold values from 0 to 991
- edge_target: int32 [8, 4, 8, 4, 128], P('gx', 'gy', 'gz'), may hold values from 0 to 127
- edge_count: int32 [8, 4, 8, 4], P('gx', 'gy', 'gz'), may hold values from 1 to 128
- block_count: int32 [8, 4, 8], P('gx', 'gy', 'gz'), may hold values from 0 to 4, as said below
- wigner: bfloat16 [8, 4, 8, 4, 165, 128], P('gx', 'gy', 'gz'), may hold values from -2.6875 to 2.6875
- w_zero: bfloat16 [2, 640, 640], replicated, may hold values from -0.25 to 0.25
- w_one: bfloat16 [2, 2, 512, 512], replicated, may hold values from -0.1875 to 0.1875
- w_two: bfloat16 [2, 2, 384, 384], replicated, may hold values from -0.21875 to 0.21875
- attn_vector: float32 [128], replicated, may hold values from -3 to 3
Outputs:
- update: bfloat16 [8, 4, 8, 128, 3200], P('gx', 'gy', 'gz')
Inputs may be any that keep to these rules, and one draw needn't show every extreme that they name: `edge_source`: rows of the home device's source table: 128 own atoms, then 27 blocks of 32. Devices 2i and 2i + 1 along gz (same gx and gy) hold 4 live blocks together; the live blocks of a home are its first block_count ones.
All inputs are finite; a program needn't handle non-finite values.
Results may differ from a plain program's by a relative error of at most 0.0079.
Values may be sent and summed in bfloat16 or wider, within the bound.
A program may use at most 128 MiB of HBM per device.

v0:
```python
import math

import jax
import jax.numpy as jnp
import numpy as np
from jax import lax
from jax.sharding import PartitionSpec as P

CH = 128
HEADS = 8


EPS = 1e-06


def with_halo(block, sides, width):
    for axis, dim in sides:
        count = lax.axis_size(axis)
        forward = [(i, i + 1) for i in range(count - 1)]
        forward.append((count - 1, 0))
        backward = [(target, source) for source, target in forward]
        low = lax.ppermute(
            lax.slice_in_dim(block, block.shape[dim] - width, None, axis=dim), axis, forward
        )
        high = lax.ppermute(lax.slice_in_dim(block, 0, width, axis=dim), axis, backward)
        block = jnp.concatenate([low, block, high], axis=dim)
    return block


def keep_index():
    ordering = [0, 2, 6, 12, 20, 3, 7, 13, 21, 1, 5, 11, 19, 8, 14, 22, 4, 10, 18]
    starts = [0, 1, 10, 35, 84]
    lookup = np.full((19, 25), 165, dtype=np.int32)
    for row_pos, component in enumerate(ordering):
        degree = math.isqrt(component)
        offset = component - degree * degree
        for column in range(2 * degree + 1):
            lookup[row_pos, degree * degree + column] = (
                starts[degree] + offset * (2 * degree + 1) + column
            )
    return lookup


def expand_frames(packed):
    padded = jnp.concatenate([packed, jnp.zeros_like(packed[:, :1])], axis=1)
    picked = jnp.take(padded, jnp.asarray(keep_index().reshape(-1)), axis=1)
    return picked.reshape(packed.shape[0], 19, 25, packed.shape[2])


def rms_norm(values):
    widened = values.astype(jnp.float32)
    factor = lax.rsqrt(jnp.mean(widened * widened, axis=-1, keepdims=True) + EPS)
    return (widened * factor).astype(jnp.bfloat16)


def product(left, right):
    return jnp.dot(left, right, preferred_element_type=jnp.float32)


def degree_mix(inputs, weight_zero, weight_one, weight_two):
    zero_out = product(inputs[:, : 5 * CH], weight_zero)
    plus_one = inputs[:, 5 * CH : 9 * CH]
    minus_one = inputs[:, 9 * CH : 13 * CH]
    plus_two = inputs[:, 13 * CH : 16 * CH]
    minus_two = inputs[:, 16 * CH :]
    one_plus = product(plus_one, weight_one[0]) - product(minus_one, weight_one[1])
    one_minus = product(minus_one, weight_one[0]) + product(plus_one, weight_one[1])
    two_plus = product(plus_two, weight_two[0]) - product(minus_two, weight_two[1])
    two_minus = product(minus_two, weight_two[0]) + product(plus_two, weight_two[1])
    return jnp.concatenate([zero_out, one_plus, one_minus, two_plus, two_minus], axis=1)


def edge_work(rotated, live_mask, w_zero, w_one, w_two, attn_vector):
    edge_total = rotated.shape[0]
    mixed_one = degree_mix(rotated, w_zero[0], w_one[0], w_two[0])
    scalars = mixed_one[:, :CH]
    logits = jnp.sum(
        (jax.nn.silu(scalars) * attn_vector).reshape(edge_total, HEADS, CH // HEADS), axis=-1
    )
    weights = jax.nn.sigmoid(logits) * live_mask[:, None]
    higher = mixed_one[:, CH:].reshape(edge_total, 18, CH) * jax.nn.sigmoid(scalars)[:, None, :]
    activated = jnp.concatenate(
        [jax.nn.silu(scalars), higher.reshape(edge_total, 18 * CH)], axis=1
    ).astype(jnp.bfloat16)
    mixed_two = degree_mix(activated, w_zero[1], w_one[1], w_two[1])
    weighted = mixed_two.reshape(edge_total, 19, HEADS, CH // HEADS) * weights[:, None, :, None]
    return weighted.reshape(edge_total, 19 * CH).astype(jnp.bfloat16)


def rotate_in(frames, gathered):
    return jnp.einsum(
        "gije,gejc->geic", frames, gathered, preferred_element_type=jnp.float32
    ).astype(jnp.bfloat16)


def rotate_out(frames, weighted):
    return jnp.einsum(
        "gije,geic->gejc", frames, weighted, preferred_element_type=jnp.float32
    ).astype(jnp.bfloat16)


def body(
    coeffs,
    halo_rows,
    edge_source,
    edge_target,
    edge_count,
    block_count,
    wigner,
    w_zero,
    w_one,
    w_two,
    attn_vector,
):
    feature_width = coeffs.shape[4]
    normed = rms_norm(coeffs[0, 0, 0])
    atom_count = normed.shape[0]
    boundary = normed[halo_rows[0, 0, 0]]
    received = with_halo(boundary[None, None, None], (("gx", 0), ("gy", 1), ("gz", 2)), 1)
    source_table = jnp.concatenate([normed, received.reshape(-1, feature_width)], axis=0)
    home_blocks = edge_source.shape[3]
    block_size = edge_source.shape[4]
    sources = edge_source[0, 0, 0]
    targets = edge_target[0, 0, 0]
    counts = edge_count[0, 0, 0]
    owned = block_count[0, 0, 0]
    packed = wigner[0, 0, 0]
    frames = expand_frames(packed)
    gathered = source_table[sources.reshape(-1)].reshape(home_blocks, block_size, 25, CH)
    home_edges = lax.broadcasted_iota(jnp.int32, (home_blocks, block_size), 1)
    home_ids = lax.broadcasted_iota(jnp.int32, (home_blocks, block_size), 0)
    live_mask = (
        ((home_edges < counts[:, None]) & (home_ids < owned)).astype(jnp.float32).reshape(-1)
    )
    rotated = rotate_in(frames, gathered)
    weighted = edge_work(
        rotated.reshape(home_blocks * block_size, 19 * CH),
        live_mask,
        w_zero,
        w_one,
        w_two,
        attn_vector,
    )
    home_messages = rotate_out(frames, weighted.reshape(home_blocks, block_size, 19, CH))
    onehot = (
        lax.broadcasted_iota(jnp.int32, (atom_count, home_blocks * block_size), 0)
        == targets.reshape(1, -1)
    ).astype(jnp.bfloat16)
    summed = jnp.dot(
        onehot,
        home_messages.reshape(home_blocks * block_size, feature_width),
        preferred_element_type=jnp.float32,
    )
    return summed.astype(jnp.bfloat16).reshape(1, 1, 1, atom_count, feature_width)


def solution(mesh):
    placed = (
        P("gx", "gy", "gz", None, None),
        P("gx", "gy", "gz", None),
        P("gx", "gy", "gz", None, None),
        P("gx", "gy", "gz", None, None),
        P("gx", "gy", "gz", None),
        P("gx", "gy", "gz"),
        P("gx", "gy", "gz", None, None, None),
        P(),
        P(),
        P(),
        P(),
    )
    return jax.shard_map(
        body, mesh=mesh, in_specs=placed, out_specs=P("gx", "gy", "gz", None, None), check_vma=False
    )
```

profile of v0, /device:TPU:1, one launch (start us, length us, event | category | flops | bytes accessed | tf_op | source)
XLA Modules:
  0.0 188.6 jit_solution(8468760391740324317)
XLA Ops:
  0.0 1.4 fusion.4
  1.4 1.4 fusion.5
  2.8 0.0 copy-start.2
  2.8 0.7 compare_select_fusion
  3.5 0.7 fusion.80
  4.1 0.6 pad_clamp_fusion
  4.7 0.7 gather_fusion.1
  5.4 0.0 copy-start.17
  5.5 3.6 %collective-permute-start = (bf16[1,1,1,32,3200]{4,3,2,1,0:T(8,128)(2,1)S(1)}, bf16[1,1,1,32,3200]{4,3,2,1,0:T(8,128)(2,1)S(1)}, u32[]{:S(2)}, u32[]{:S(2)}) collective-permute-start(bf16[1,1,1,32,3200]{4,3,2,1,0:T(8,128)(2,1)S(1)} %bitcast.108), channel_id=1, source_target_pairs={{0,32},{32,64},{64,96},{96,128},{128,160},{160,192},{192,224},{224... | collective-permute-start | bytes 614408 | tf_op jit(solution)/shard_map/ppermute | solution.py:22
  9.1 2.5 %collective-permute-start.1 = (bf16[1,1,1,32,3200]{4,3,2,1,0:T(8,128)(2,1)S(1)}, bf16[1,1,1,32,3200]{4,3,2,1,0:T(8,128)(2,1)S(1)}, u32[]{:S(2)}, u32[]{:S(2)}) collective-permute-start(bf16[1,1,1,32,3200]{4,3,2,1,0:T(8,128)(2,1)S(1)} %bitcast.109), channel_id=1, source_target_pairs={{32,0},{64,32},{96,64},{128,96},{160,128},{192,160},{224,192},{0,2... | collective-permute-start | bytes 614408 | tf_op jit(solution)/shard_map/ppermute | solution.py:25
  11.6 3.1 %collective-permute-done = bf16[1,1,1,32,3200]{4,3,2,1,0:T(8,128)(2,1)S(1)} collective-permute-done((bf16[1,1,1,32,3200]{4,3,2,1,0:T(8,128)(2,1)S(1)}, bf16[1,1,1,32,3200]{4,3,2,1,0:T(8,128)(2,1)S(1)}, u32[]{:S(2)}, u32[]{:S(2)}) %collective-permute-start) | collective-permute-done | bytes 204832 | tf_op jit(solution)/shard_map/ppermute | solution.py:22
  14.7 4.5 %collective-permute-done.1 = bf16[1,1,1,32,3200]{4,3,2,1,0:T(8,128)(2,1)S(1)} collective-permute-done((bf16[1,1,1,32,3200]{4,3,2,1,0:T(8,128)(2,1)S(1)}, bf16[1,1,1,32,3200]{4,3,2,1,0:T(8,128)(2,1)S(1)}, u32[]{:S(2)}, u32[]{:S(2)}) %collective-permute-start.1) | collective-permute-done | bytes 204832 | tf_op jit(solution)/shard_map/ppermute | solution.py:25
  19.2 0.1 pad_maximum_fusion.5
  19.3 2.7 %collective-permute-start.2 = (bf16[3,1,1,32,3200]{4,3,2,1,0:T(8,128)(2,1)S(1)}, bf16[3,1,1,32,3200]{4,3,2,1,0:T(8,128)(2,1)S(1)}, u32[]{:S(2)}, u32[]{:S(2)}) collective-permute-start(bf16[3,1,1,32,3200]{4,3,2,1,0:T(8,128)(2,1)S(1)} %pad_maximum_fusion.5), channel_id=1, source_target_pairs={{0,8},{8,16},{16,24},{24,0},{1,9},{9,17},{17,25},{25,1},{2,10},{10... | collective-permute-start | bytes 1843208 | tf_op jit(solution)/shard_map/ppermute | solution.py:22
  22.0 12.8 %collective-permute-done.2 = bf16[3,1,1,32,3200]{4,3,2,1,0:T(8,128)(2,1)S(1)} collective-permute-done((bf16[3,1,1,32,3200]{4,3,2,1,0:T(8,128)(2,1)S(1)}, bf16[3,1,1,32,3200]{4,3,2,1,0:T(8,128)(2,1)S(1)}, u32[]{:S(2)}, u32[]{:S(2)}) %collective-permute-start.2) | collective-permute-done | bytes 614432 | tf_op jit(solution)/shard_map/ppermute | solution.py:22
  34.9 1.5 collective-permute-done.3
  36.4 1.5 pad_maximum_fusion.2
  37.9 1.6 collective-permute-start.4
  39.6 3.9 %collective-permute-start.5 = (bf16[3,3,1,32,3200]{4,3,2,1,0:T(8,128)(2,1)}, bf16[3,3,1,32,3200]{4,3,2,1,0:T(8,128)(2,1)}, u32[]{:S(2)}, u32[]{:S(2)}) collective-permute-start(bf16[3,3,1,32,3200]{4,3,2,1,0:T(8,128)(2,1)} %pad_maximum_fusion.2), channel_id=1, source_target_pairs={{1,0},{2,1},{3,2},{4,3},{5,4},{6,5},{7,6},{0,7},{9,8},{10,9},{11,1... | collective-permute-start | bytes 5529608 | tf_op jit(solution)/shard_map/ppermute | solution.py:25
  43.5 0.1 concatenate.27
  43.6 2.5 %gather_fusion = bf16[475,4,128]{2,1,0:T(4,128)(2,1)} fusion(bf16[4,166,128]{2,0,1:T(4,128)(2,1)S(1)} %concatenate.27, s32[1024]{0:T(1024)S(1)} %pad_clamp_fusion.2), kind=kCustom, calls=%fused_computation | custom fusion | bytes 974700 | tf_op jit(solution)/shard_map/jit(_take)/gather | solution.py:46
  46.1 3.2 %copy.55 = bf16[4,19,25,128]{2,1,3,0:T(8,128)(2,1)S(1)} copy(bf16[4,19,25,128]{3,0,2,1:T(4,128)(2,1)} %bitcast.113) | data formatting | bytes 972800 | tf_op jit(solution)/shard_map/jit(_take)/gather | solution.py:46
  50.0 1.3 convert_bitcast_fusion
  51.3 33.0 %collective-permute-done.4 = bf16[3,3,1,32,3200]{4,3,2,1,0:T(8,128)(2,1)} collective-permute-done((bf16[3,3,1,32,3200]{4,3,2,1,0:T(8,128)(2,1)}, bf16[3,3,1,32,3200]{4,3,2,1,0:T(8,128)(2,1)}, u32[]{:S(2)}, u32[]{:S(2)}) %collective-permute-start.4) | collective-permute-done | bytes 1843232 | tf_op jit(solution)/shard_map/ppermute | solution.py:22
  84.3 3.7 %pad_maximum_fusion.1 = bf16[3,3,3,32,3200]{4,3,2,1,0:T(8,128)(2,1)S(1)} fusion(bf16[3,3,1,32,3200]{4,3,2,1,0:T(8,128)(2,1)} %collective-permute-done.5, bf16[3,1,1,32,3200]{4,3,2,1,0:T(8,128)(2,1)} %copy-done.10, bf16[1,1,1,32,3200]{4,3,2,1,0:T(8,128)(2,1)} %copy-done.11, bf16[1,1,1,32,3200]{4,3,2,1,0:T(8,128)(2,1)S(1)} %bitcast.112, ...), kind=kLoop, calls=%fused_computation.4 | loop fusion | flops 16588800 | bytes 11059200 | tf_op jit(solution)/shard_map/concatenate | solution.py:26
  88.0 3.1 %pad_maximum_fusion = bf16[992,3200]{1,0:T(8,128)(2,1)} fusion(bf16[864,3200]{1,0:T(8,128)(2,1)S(1)} %bitcast.93, bf16[128,3200]{1,0:T(8,128)(2,1)S(1)} %copy-done.3), kind=kLoop, calls=%fused_computation.3 | loop fusion | flops 12697600 | bytes 12697600 | tf_op jit(solution)/shard_map/concatenate | solution.py:120
  91.1 10.9 %gather_fusion.2 = bf16[512,3200]{1,0:T(8,128)(2,1)} fusion(bf16[992,3200]{1,0:T(8,128)(2,1)} %pad_maximum_fusion, s32[1024]{0:T(1024)S(1)} %copy-done.15), kind=kCustom, calls=%fused_computation.2 | custom fusion | bytes 6555648 | tf_op jit(solution)/shard_map/gather | solution.py:129
  102.0 6.7 %reshape.201 = bf16[4,128,25,128]{3,2,1,0:T(8,128)(2,1)} reshape(bf16[512,3200]{1,0:T(8,128)(2,1)} %gather_fusion.2) | data formatting | bytes 6553600 | tf_op jit(solution)/shard_map/reshape | solution.py:129
  108.8 4.5 %convolution_convert_fusion.2 = bf16[4,128,19,128]{3,2,1,0:T(8,128)(2,1)S(1)} fusion(bf16[4,19,25,128]{2,1,3,0:T(8,128)(2,1)S(1)} %copy.55, bf16[4,128,25,128]{3,2,1,0:T(8,128)(2,1)} %reshape.201), kind=kOutput, calls=%fused_computation.14 | convolution fusion | flops 63504384 | bytes 6253568 | tf_op jit(solution)/shard_map/gije,gejc->geic/dot_general | solution.py:91
  113.2 0.4 copy.89
  113.7 1.7 copy-done.4
  115.3 1.4 fusion.31
  116.7 1.4 fusion.29
  118.1 1.3 fusion.58
  119.4 1.3 fusion.56
  120.7 1.8 constant_dynamic-update-slice_fusion
  122.5 0.8 broadcast_multiply_fusion
  123.3 1.8 copy.43
  125.1 3.8 %mul.65 = f32[512,18,128]{0,2,1:T(8,128)} broadcast(f32[512,128]{0,1:T(8,128)} %copy.43), dimensions={0,2} | broadcast | bytes 4980736 | tf_op jit(solution)/shard_map/mul | solution.py:81
  128.9 6.1 %copy.44 = f32[512,2304]{1,0:T(8,128)} copy(f32[512,2304]{0,1:T(8,128)} %bitcast.94) | data formatting | bytes 9437184 | tf_op jit(solution)/shard_map/mul | solution.py:81
  135.0 3.1 %fusion.9 = f32[512,2432]{1,0:T(8,128)} fusion(f32[512,2432]{1,0:T(8,128)} %get-tuple-element.8, f32[512,512]{1,0:T(8,128)} %fusion.31, bf16[512,2432]{1,0:T(8,128)(2,1)} %bitcast.102, bf16[2,2,512,512]{3,2,1,0:T(8,128)(2,1)} %param.20), kind=kOutput, calls=%fused_computation.28 | convolution fusion | flops 268697600 | bytes 3145728 | tf_op jit(solution)/shard_map/dot_general | solution.py:57
  138.1 3.3 %fusion.8 = f32[512,2432]{1,0:T(8,128)} fusion(f32[512,2432]{1,0:T(8,128)} %fusion.9, f32[512,512]{1,0:T(8,128)} %fusion.29, bf16[512,2432]{1,0:T(8,128)(2,1)S(1)} %bitcast.103, bf16[2,2,512,512]{3,2,1,0:T(8,128)(2,1)} %param.20), kind=kOutput, calls=%fused_computation.26 | convolution fusion | flops 268697600 | bytes 3145728 | tf_op jit(solution)/shard_map/dot_general | solution.py:57
  141.4 1.3 fusion.13
  142.8 2.4 %fusion.12 = f32[512,2432]{1,0:T(8,128)} fusion(f32[512,2432]{1,0:T(8,128)} %fusion.13, f32[512,384]{1,0:T(8,128)} %fusion.56, bf16[512,2432]{1,0:T(8,128)(2,1)S(1)} %bitcast.105, bf16[2,2,384,384]{3,2,1,0:T(8,128)(2,1)S(1)} %copy-done.7), kind=kOutput, calls=%fused_computation.34 | convolution fusion | flops 151191552 | bytes 2260992 | tf_op jit(solution)/shard_map/dot_general | solution.py:57
  145.2 3.1 %fusion = bf16[512,2304]{1,0:T(8,128)(2,1)S(1)} fusion(f32[512,2304]{1,0:T(8,128)S(1)} %bitcast.96, f32[512,2432]{1,0:T(8,128)} %fusion.12), kind=kLoop, calls=%fused_computation.8 | loop fusion | flops 2359296 | bytes 11796480 | tf_op jit(solution)/shard_map/convert.3
  148.3 0.4 fusion.25
  148.7 0.4 fusion.23
  149.2 0.4 fusion.53
  149.6 0.4 fusion.49
  150.0 0.2 copy-done.13
  150.1 1.8 convolution_dynamic-update-slice_fusion
  152.0 1.4 fusion.7
  153.4 1.5 fusion.6
  154.9 1.3 fusion.11
  156.3 1.3 fusion.10
  157.6 5.9 %copy.53 = f32[512,2432]{0,1:T(8,128)} copy(f32[512,2432]{1,0:T(8,128)} %fusion.10) | data formatting | bytes 9961472 | tf_op jit(solution)/shard_map/concatenate | solution.py:70
  163.5 6.8 %concatenate.35 = f32[4,128,19,128]{1,0,3,2:T(4,128)} reshape(f32[512,2432]{0,1:T(8,128)} %copy.53) | data formatting | bytes 9961472 | tf_op jit(solution)/shard_map/concatenate | solution.py:70
  170.3 0.8 copy.54
  171.1 1.0 bitcast_reduce_fusion
  172.2 0.8 mul.73
  173.0 4.9 %multiply_convert_fusion = bf16[4,128,19,128]{1,0,3,2:T(4,128)(2,1)} fusion(f32[4,128,19,128]{1,0,3,2:T(4,128)} %concatenate.35, f32[4,128,128]{1,0,2:T(4,128)} %mul.73), kind=kLoop, calls=%fused_computation.5 | loop fusion | flops 2490368 | bytes 7733248 | tf_op jit(solution)/shard_map/convert_element_type | solution.py:87
  177.9 5.0 %copy.56 = bf16[4,128,19,128]{3,2,1,0:T(8,128)(2,1)} copy(bf16[4,128,19,128]{1,0,3,2:T(4,128)(2,1)} %multiply_convert_fusion) | data formatting | bytes 4980736 | tf_op jit(solution)/shard_map/convert_element_type | solution.py:87
  182.9 3.4 %convolution_convert_fusion.1 = bf16[4,128,25,128]{3,2,1,0:T(8,128)(2,1)S(1)} fusion(bf16[4,19,25,128]{2,1,3,0:T(8,128)(2,1)S(1)} %copy.55, bf16[4,128,19,128]{3,2,1,0:T(8,128)(2,1)} %copy.56), kind=kOutput, calls=%fused_computation.12 | convolution fusion | flops 63897600 | bytes 6253568 | tf_op jit(solution)/shard_map/gije,geic->gejc/dot_general | solution.py:97
  186.3 2.3 %fusion.1 = bf16[1,1,1,128,3200]{4,3,2,1,0:T(8,128)(2,1)} fusion(bf16[64,8,25,128]{3,2,1,0:T(8,128)(2,1)S(1)} %bitcast.107, s32[512]{0:T(512)S(1)} %bitcast.118), kind=kOutput, calls=%fused_computation.9 | convolution fusion | flops 419905536 | bytes 4098048 | tf_op jit(solution)/shard_map/dot_general | solution.py:149
  (48 shorter events, 0.1 us)
Async XLA Ops:
  2.8 35.2 %copy-start.2 = (bf16[128,3200]{1,0:T(8,128)(2,1)}, bf16[128,3200]{1,0:T(8,128)(2,1)S(1)}, u32[]{:S(2)}) copy-start(bf16[128,3200]{1,0:T(8,128)(2,1)S(1)} %fusion.5) | copy-start | bytes 2457604
  5.4 38.1 %copy-start.14 = (bf16[1,1,1,4,165,128]{5,3,4,2,1,0:T(4,128)(2,1)S(1)}, bf16[1,1,1,4,165,128]{5,3,4,2,1,0:T(4,128)(2,1)}, u32[]{:S(2)}) copy-start(bf16[1,1,1,4,165,128]{5,3,4,2,1,0:T(4,128)(2,1)} %param.18) | copy-start | bytes 506884
  5.4 38.1 %copy-start.17 = (s32[475]{0:T(512)S(1)}, s32[475]{0:T(512)}, u32[]{:S(2)}) copy-start(s32[475]{0:T(512)} %constant.58) | copy-start | bytes 5704
  5.5 9.2 %collective-permute-start = (bf16[1,1,1,32,3200]{4,3,2,1,0:T(8,128)(2,1)S(1)}, bf16[1,1,1,32,3200]{4,3,2,1,0:T(8,128)(2,1)S(1)}, u32[]{:S(2)}, u32[]{:S(2)}) collective-permute-start(bf16[1,1,1,32,3200]{4,3,2,1,0:T(8,128)(2,1)S(1)} %bitcast.108), channel_id=1, source_target_pairs={{0,32},{32,64},{64,96},{96,128},{128,160},{160,192},{192,224},{224... | collective-permute-start | bytes 614408 | tf_op jit(solution)/shard_map/ppermute | solution.py:22
  9.1 10.1 %collective-permute-start.1 = (bf16[1,1,1,32,3200]{4,3,2,1,0:T(8,128)(2,1)S(1)}, bf16[1,1,1,32,3200]{4,3,2,1,0:T(8,128)(2,1)S(1)}, u32[]{:S(2)}, u32[]{:S(2)}) collective-permute-start(bf16[1,1,1,32,3200]{4,3,2,1,0:T(8,128)(2,1)S(1)} %bitcast.109), channel_id=1, source_target_pairs={{32,0},{64,32},{96,64},{128,96},{160,128},{192,160},{224,192},{0,2... | collective-permute-start | bytes 614408 | tf_op jit(solution)/shard_map/ppermute | solution.py:25
  19.2 24.4 %copy-start.11 = (bf16[1,1,1,32,3200]{4,3,2,1,0:T(8,128)(2,1)}, bf16[1,1,1,32,3200]{4,3,2,1,0:T(8,128)(2,1)S(1)}, u32[]{:S(2)}) copy-start(bf16[1,1,1,32,3200]{4,3,2,1,0:T(8,128)(2,1)S(1)} %collective-permute-done.1) | copy-start | bytes 614404
  19.3 15.5 %collective-permute-start.2 = (bf16[3,1,1,32,3200]{4,3,2,1,0:T(8,128)(2,1)S(1)}, bf16[3,1,1,32,3200]{4,3,2,1,0:T(8,128)(2,1)S(1)}, u32[]{:S(2)}, u32[]{:S(2)}) collective-permute-start(bf16[3,1,1,32,3200]{4,3,2,1,0:T(8,128)(2,1)S(1)} %pad_maximum_fusion.5), channel_id=1, source_target_pairs={{0,8},{8,16},{16,24},{24,0},{1,9},{9,17},{17,25},{25,1},{2,10},{10... | collective-permute-start | bytes 1843208 | tf_op jit(solution)/shard_map/ppermute | solution.py:22
  22.0 14.4 %collective-permute-start.3 = (bf16[3,1,1,32,3200]{4,3,2,1,0:T(8,128)(2,1)S(1)}, bf16[3,1,1,32,3200]{4,3,2,1,0:T(8,128)(2,1)S(1)}, u32[]{:S(2)}, u32[]{:S(2)}) collective-permute-start(bf16[3,1,1,32,3200]{4,3,2,1,0:T(8,128)(2,1)S(1)} %pad_maximum_fusion.5), channel_id=1, source_target_pairs={{8,0},{16,8},{24,16},{0,24},{9,1},{17,9},{25,17},{1,25},{10,2},{18... | collective-permute-start | bytes 1843208 | tf_op jit(solution)/shard_map/ppermute | solution.py:25
  34.9 11.3 %copy-start.9 = (bf16[3,1,1,32,3200]{4,3,2,1,0:T(8,128)(2,1)}, bf16[3,1,1,32,3200]{4,3,2,1,0:T(8,128)(2,1)S(1)}, u32[]{:S(2)}) copy-start(bf16[3,1,1,32,3200]{4,3,2,1,0:T(8,128)(2,1)S(1)} %collective-permute-done.2) | copy-start | bytes 1843204
  36.4 9.8 %copy-start.10 = (bf16[3,1,1,32,3200]{4,3,2,1,0:T(8,128)(2,1)}, bf16[3,1,1,32,3200]{4,3,2,1,0:T(8,128)(2,1)S(1)}, u32[]{:S(2)}) copy-start(bf16[3,1,1,32,3200]{4,3,2,1,0:T(8,128)(2,1)S(1)} %collective-permute-done.3) | copy-start | bytes 1843204
  37.9 46.4 %collective-permute-start.4 = (bf16[3,3,1,32,3200]{4,3,2,1,0:T(8,128)(2,1)}, bf16[3,3,1,32,3200]{4,3,2,1,0:T(8,128)(2,1)}, u32[]{:S(2)}, u32[]{:S(2)}) collective-permute-start(bf16[3,3,1,32,3200]{4,3,2,1,0:T(8,128)(2,1)} %pad_maximum_fusion.2), channel_id=1, source_target_pairs={{0,1},{1,2},{2,3},{3,4},{4,5},{5,6},{6,7},{7,0},{8,9},{9,10},{10,1... | collective-permute-start | bytes 5529608 | tf_op jit(solution)/shard_map/ppermute | solution.py:22
  39.6 44.8 %collective-permute-start.5 = (bf16[3,3,1,32,3200]{4,3,2,1,0:T(8,128)(2,1)}, bf16[3,3,1,32,3200]{4,3,2,1,0:T(8,128)(2,1)}, u32[]{:S(2)}, u32[]{:S(2)}) collective-permute-start(bf16[3,3,1,32,3200]{4,3,2,1,0:T(8,128)(2,1)} %pad_maximum_fusion.2), channel_id=1, source_target_pairs={{1,0},{2,1},{3,2},{4,3},{5,4},{6,5},{7,6},{0,7},{9,8},{10,9},{11,1... | collective-permute-start | bytes 5529608 | tf_op jit(solution)/shard_map/ppermute | solution.py:25
  51.3 36.7 %copy-start.3 = (bf16[128,3200]{1,0:T(8,128)(2,1)S(1)}, bf16[128,3200]{1,0:T(8,128)(2,1)}, u32[]{:S(2)}) copy-start(bf16[128,3200]{1,0:T(8,128)(2,1)} %copy-done.2) | copy-start | bytes 2457604
  88.0 3.1 %copy-start.15 = (s32[1024]{0:T(1024)S(1)}, s32[1024]{0:T(1024)}, u32[]{:S(2)}) copy-start(s32[1024]{0:T(1024)} %get-tuple-element.10) | copy-start | bytes 12292
  113.2 2.1 %copy-start.4 = (bf16[2,2,512,512]{3,2,1,0:T(8,128)(2,1)S(1)}, bf16[2,2,512,512]{3,2,1,0:T(8,128)(2,1)}, u32[]{:S(2)}) copy-start(bf16[2,2,512,512]{3,2,1,0:T(8,128)(2,1)} %param.20) | copy-start | bytes 6291460
  113.6 7.1 %copy-start = (bf16[64,8,19,128]{3,1,2,0:T(8,128)(2,1)}, bf16[64,8,19,128]{3,1,2,0:T(8,128)(2,1)S(1)}, u32[]{:S(2)}) copy-start(bf16[64,8,19,128]{3,1,2,0:T(8,128)(2,1)S(1)} %copy.89) | copy-start | bytes 7471108
  113.6 4.5 %copy-start.6 = (bf16[2,2,384,384]{3,2,1,0:T(8,128)(2,1)S(1)}, bf16[2,2,384,384]{3,2,1,0:T(8,128)(2,1)}, u32[]{:S(2)}) copy-start(bf16[2,2,384,384]{3,2,1,0:T(8,128)(2,1)} %param.21) | copy-start | bytes 3538948
  116.7 4.0 %copy-start.12 = (bf16[2,640,640]{2,1,0:T(8,128)(2,1)S(1)}, bf16[2,640,640]{2,1,0:T(8,128)(2,1)}, u32[]{:S(2)}) copy-start(bf16[2,640,640]{2,1,0:T(8,128)(2,1)} %param.19) | copy-start | bytes 4915204
  119.4 3.1 %copy-start.18 = (f32[128]{0:T(128)S(1)}, f32[128]{0:T(128)}, u32[]{:S(2)}) copy-start(f32[128]{0:T(128)} %param.22) | copy-start | bytes 1540
  135.0 3.2 %copy-start.1 = (bf16[64,8,19,128]{3,1,2,0:T(8,128)(2,1)S(1)}, bf16[64,8,19,128]{3,1,2,0:T(8,128)(2,1)}, u32[]{:S(2)}) copy-start(bf16[64,8,19,128]{3,1,2,0:T(8,128)(2,1)} %copy-done) | copy-start | bytes 7471108
  135.0 6.4 %copy-start.7 = (bf16[2,2,384,384]{3,2,1,0:T(8,128)(2,1)S(1)}, bf16[2,2,384,384]{3,2,1,0:T(8,128)(2,1)}, u32[]{:S(2)}) copy-start(bf16[2,2,384,384]{3,2,1,0:T(8,128)(2,1)} %param.21) | copy-start | bytes 3538948
  135.0 6.4 %copy-start.8 = (f32[512,384]{1,0:T(8,128)S(1)}, f32[512,384]{1,0:T(8,128)}, u32[]{:S(2)}) copy-start(f32[512,384]{1,0:T(8,128)} %fusion.58) | copy-start | bytes 2359300
  135.0 10.2 %slice-start = ((s8[4718592]{0:T(1024)(128)(4,1)}), s8[4194304]{0:T(1024)(128)(4,1)S(1)}, s32[]{:S(2)}) async-start(s8[4718592]{0:T(1024)(128)(4,1)} %bitcast.95), calls=%async_computation | async-start | bytes 8388608
  138.1 7.0 %slice-start.1 = ((s8[4718592]{0:T(1024)(128)(4,1)}), s8[524288]{0:T(1024)(128)(4,1)S(1)}, s32[]{:S(2)}) async-start(s8[4718592]{0:T(1024)(128)(4,1)} %bitcast.95), calls=%async_computation.1 | async-start | bytes 1048576
  145.2 3.1 %copy-start.5 = (bf16[2,2,512,512]{3,2,1,0:T(8,128)(2,1)S(1)}, bf16[2,2,512,512]{3,2,1,0:T(8,128)(2,1)}, u32[]{:S(2)}) copy-start(bf16[2,2,512,512]{3,2,1,0:T(8,128)(2,1)} %param.20) | copy-start | bytes 6291460
  148.7 1.4 copy-start.13
  163.5 8.6 %copy-start.16 = (f32[512]{0:T(512)S(1)}, f32[512]{0:T(512)}, u32[]{:S(2)}) copy-start(f32[512]{0:T(512)} %convert_bitcast_fusion) | copy-start | bytes 6148
  182.9 3.4 %copy-start.19 = (s32[1,1,1,4,128]{4,3,2,1,0:T(4,128)S(1)}, s32[1,1,1,4,128]{4,3,2,1,0:T(4,128)}, u32[]{:S(2)}) copy-start(s32[1,1,1,4,128]{4,3,2,1,0:T(4,128)} %param.15) | copy-start | bytes 6148
where the time goes:
time: 189 us
  local copies, waits for them, and re-layouts  57.5 us (30%)
  waiting for transfers between devices  54.9 us (29%)
  matrix products  36.6 us (19%)
  other arithmetic  24.2 us (13%)
  starting transfers between devices  14.5 us (8%)
    ppermute x3, waiting for transfers between devices, with_halo(): lax.ppermute(lax.slice_in_dim(block, block.shape[dim] - width, None, axis...  48.9 us
    dot_general x18, matrix products, product(): return jnp.dot(left, right, preferred_element_type=jnp.float32)  26.5 us
    concatenate x2, local copies, waits for them, and re-layouts, degree_mix(): jnp.concatenate([zero_out, one_plus, one_minus, two_plus, two_minus], axi...  12.7 us
    gather x1, local copies, waits for them, and re-layouts, body(): source_table[sources.reshape(-1)].reshape(home_blocks, block_size, 25, CH)  10.9 us
    mul x2, local copies, waits for them, and re-layouts, edge_work(): mixed_one[:, CH:].reshape(edge_total, 18, CH)  9.86 us
    ppermute x3, starting transfers between devices, with_halo(): lax.ppermute(lax.slice_in_dim(block, block.shape[dim] - width, None, axis...  7.99 us
    reshape x1, local copies, waits for them, and re-layouts, body(): source_table[sources.reshape(-1)].reshape(home_blocks, block_size, 25, CH)  6.72 us
    ppermute x3, starting transfers between devices, with_halo(): lax.ppermute(lax.slice_in_dim(block, 0, width, axis=dim), axis, backward)  6.48 us
  transfers between devices with their start and end apart: 6, of which 5 were waited for; matrix products, arithmetic and copies ran while one was open for 4% of the time, Pallas kernels for 0%

commit v1 on v0

v1 whole, which is shorter than its diff:
```python
import math
import functools
import jax, jax.numpy as jnp, numpy as np
from jax import lax
from jax.experimental import pallas as pl
from jax.experimental.pallas import tpu as pltpu
from jax.sharding import PartitionSpec as P

CH = 128
F32 = jnp.float32
BF16 = jnp.bfloat16
STARTS = [0, 1, 10, 35, 84]
ORDER = [0, 2, 6, 12, 20, 3, 7, 13, 21, 1, 5, 11, 19, 8, 14, 22, 4, 10, 18]
ROWS = []
for l in range(5):
    rows = []
    for pos, comp in enumerate(ORDER):
        if math.isqrt(comp) == l:
            off = comp - l * l
            rows.append((pos, [STARTS[l] + off * (2 * l + 1) + j for j in range(2 * l + 1)]))
    ROWS.append(rows)
USED = sorted({p for rows in ROWS for _, ps in rows for p in ps})
SLOT = {p: i for i, p in enumerate(USED)}
NE = 512


def bcast_frames(wig_ref, wb):
    for g in range(4):
        for i, p in enumerate(USED):
            row = wig_ref[g, p:p + 1, :].astype(F32)
            wb[i, :, g * 128:(g + 1) * 128] = jnp.broadcast_to(row, (8, 128))


def build_weights(wz, w1, w2, wzt, w1t, w2t):
    for v in range(2):
        for a in range(5):
            for b in range(5):
                wzt[v, b * CH:(b + 1) * CH, a * CH:(a + 1) * CH] = wz[v, a * CH:(a + 1) * CH, b * CH:(b + 1) * CH].T
        for (src, dst, n) in ((w1, w1t, 4), (w2, w2t, 3)):
            for a in range(n):
                for b in range(n):
                    re = src[v, 0, a * CH:(a + 1) * CH, b * CH:(b + 1) * CH].T
                    im = src[v, 1, a * CH:(a + 1) * CH, b * CH:(b + 1) * CH].T
                    dst[v, b * CH:(b + 1) * CH, a * CH:(a + 1) * CH] = re
                    dst[v, (n + b) * CH:(n + b + 1) * CH, (n + a) * CH:(n + a + 1) * CH] = re
                    dst[v, b * CH:(b + 1) * CH, (n + a) * CH:(n + a + 1) * CH] = -im
                    dst[v, (n + b) * CH:(n + b + 1) * CH, a * CH:(a + 1) * CH] = im


def transpose_table(tab, tabt):
    def step(k, _):
        c = pl.multiple_of(k * 128, 128)
        for g in range(8):
            tabt[pl.ds(c, 128), g * 128:(g + 1) * 128] = tab[g * 128:(g + 1) * 128, pl.ds(c, 128)].T
        return 0
    lax.fori_loop(0, 25, step, 0)


def rotate_in(l, gl, wb, rot):
    d = 2 * l + 1
    def step(it, _):
        e = pl.multiple_of((it % 4) * 128, 128)
        c = pl.multiple_of((it // 4) * 16, 16)
        outs = [[], [], [], [], []]
        for h in range(2):
            g = [gl[pl.ds(j * CH + c + 8 * h, 8), pl.ds(e, 128)] for j in range(d)]
            for n, (pos, ps) in enumerate(ROWS[l]):
                acc = None
                for j in range(d):
                    t = wb[SLOT[ps[j]], :, pl.ds(e, 128)] * g[j]
                    acc = t if acc is None else acc + t
                outs[n].append(acc)
        for n, (pos, ps) in enumerate(ROWS[l]):
            rot[pl.ds(pos * CH + c, 16), pl.ds(e, 128)] = jnp.concatenate(outs[n], axis=0).astype(BF16)
        return 0
    lax.fori_loop(0, 32, step, 0)


def rotate_out(l, wei, wb, msg):
    d = 2 * l + 1
    def step(it, _):
        e = pl.multiple_of((it % 4) * 128, 128)
        c = pl.multiple_of((it // 4) * 16, 16)
        w = [wei[pl.ds(pos * CH + c, 16), pl.ds(e, 128)].astype(F32) for pos, _ in ROWS[l]]
        for j in range(d):
            halves = []
            for h in range(2):
                acc = None
                for n, (pos, ps) in enumerate(ROWS[l]):
                    t = wb[SLOT[ps[j]], :, pl.ds(e, 128)] * w[n][8 * h:8 * h + 8]
                    acc = t if acc is None else acc + t
                halves.append(acc)
            msg[pl.ds(j * CH + c, 16), pl.ds(e, 128)] = jnp.concatenate(halves, axis=0).astype(BF16)
        return 0
    lax.fori_loop(0, 32, step, 0)


def dot(a, b):
    return jnp.dot(a, b, preferred_element_type=F32)


def conv_parts(v, x, wzt, w1t, w2t, emit):
    emit(0, 1, dot(wzt[v, 0:128, :], x[0:640, :]))
    emit(1, 2, dot(wzt[v, 128:384, :], x[0:640, :]))
    emit(3, 2, dot(wzt[v, 384:640, :], x[0:640, :]))
    for b in range(4):
        emit(5 + 2 * b, 2, dot(w1t[v, b * 256:(b + 1) * 256, :], x[640:1664, :]))
    for b in range(3):
        emit(13 + 2 * b, 2, dot(w2t[v, b * 256:(b + 1) * 256, :], x[1664:2432, :]))


def compute(src, tgt, cnt, blocks, attn_ref, tabt, wb, wzt, w1t, w2t, rowid, out, oh, gl, rot, act, wei, msg, attb, sigs):
    for g in range(4):
        oh[:, g * 128:(g + 1) * 128] = jnp.where(rowid == src[g:g + 1, :], 1.0, 0.0).astype(BF16)
    for l in range(5):
        d = 2 * l + 1
        for j in range(d):
            gl[j * CH:(j + 1) * CH, :] = dot(tabt[(l * l + j) * CH:(l * l + j + 1) * CH, :], oh[...])
        rotate_in(l, gl, wb, rot)

    attn = jnp.broadcast_to(attn_ref[...].reshape(1, 128), (128, 128)).T

    def emit1(c0, n, val):
        if c0 == 0:
            sig = jax.nn.sigmoid(val)
            sigs[...] = sig
            silu = val * sig
            act[0:128, :] = silu.astype(BF16)
            for g in range(4):
                t = (silu[:, g * 128:(g + 1) * 128] * attn).reshape(8, 16, 128)
                logit = jnp.sum(t, axis=1)
                edge = lax.broadcasted_iota(jnp.int32, (8, 128), 1)
                live = jnp.logical_and(edge < cnt[g], g < blocks)
                a = jnp.where(live, jax.nn.sigmoid(logit), 0.0)
                attb[:, g * 128:(g + 1) * 128] = jnp.broadcast_to(a[:, None, :], (8, 16, 128)).reshape(128, 128)
        else:
            for k in range(n):
                act[(c0 + k) * CH:(c0 + k + 1) * CH, :] = (val[k * CH:(k + 1) * CH] * sigs[...]).astype(BF16)
    conv_parts(0, rot, wzt, w1t, w2t, emit1)

    def emit2(c0, n, val):
        for k in range(n):
            wei[(c0 + k) * CH:(c0 + k + 1) * CH, :] = (val[k * CH:(k + 1) * CH] * attb[...]).astype(BF16)
    conv_parts(1, act, wzt, w1t, w2t, emit2)

    ot = []
    for g in range(4):
        atom = lax.broadcasted_iota(jnp.int32, (128, 128), 0)
        ot.append(jnp.where(atom == tgt[g:g + 1, :], 1.0, 0.0).astype(BF16))
    ot = jnp.concatenate(ot, axis=1)
    for l in range(5):
        d = 2 * l + 1
        rotate_out(l, wei, wb, msg)
        upd = lax.dot_general(ot, msg[0:d * CH, :], (((1,), (1,)), ((), ())), preferred_element_type=F32)
        out[:, l * l * CH:(l + 1) * (l + 1) * CH] = upd.astype(BF16)


COMPUTE_SCRATCH = [
    pltpu.VMEM((1024, NE), BF16),
    pltpu.VMEM((9 * CH, NE), F32),
    pltpu.VMEM((19 * CH, NE), BF16),
    pltpu.VMEM((19 * CH, NE), BF16),
    pltpu.VMEM((19 * CH, NE), BF16),
    pltpu.VMEM((9 * CH, NE), BF16),
    pltpu.VMEM((CH, NE), F32),
    pltpu.VMEM((CH, NE), F32),
]
PREP_SCRATCH = [
    pltpu.VMEM((3200, 1024), BF16),
    pltpu.VMEM((115, 8, NE), F32),
    pltpu.VMEM((2, 640, 640), BF16),
    pltpu.VMEM((2, 1024, 1024), BF16),
    pltpu.VMEM((2, 768, 768), BF16),
]


def v1_kernel(cnt, blocks, tab, src, tgt, wig, wz, w1, w2, attn, out, tabt, wb, wzt, w1t, w2t, tabp, *scr):
    bcast_frames(wig, wb)
    build_weights(wz, w1, w2, wzt, w1t, w2t)
    tabp[0:992, :] = tab[...]
    tabp[992:1024, :] = jnp.zeros((32, 3200), BF16)
    transpose_table(tabp, tabt)
    rowid = lax.broadcasted_iota(jnp.int32, (1024, 1), 0)
    compute(src, tgt, cnt, blocks[0], attn, tabt, wb, wzt, w1t, w2t, rowid, out, *scr)


def v1_call(tab, src, tgt, cnt, blocks, wig, wz, w1, w2, attn):
    vm = pl.BlockSpec(memory_space=pltpu.VMEM)
    sm = pl.BlockSpec(memory_space=pltpu.SMEM)
    return pl.pallas_call(
        v1_kernel,
        out_shape=jax.ShapeDtypeStruct((128, 3200), BF16),
        in_specs=[sm, sm] + [vm] * 8,
        out_specs=vm,
        scratch_shapes=PREP_SCRATCH + [pltpu.VMEM((1024, 3200), BF16)] + COMPUTE_SCRATCH,
        compiler_params=pltpu.CompilerParams(vmem_limit_bytes=67043328),
    )(cnt, blocks, tab, src, tgt, wig, wz, w1, w2, attn.reshape(1, 128))


EPS = 1e-06


def with_halo(block, sides, width):
    for axis, dim in sides:
        count = lax.axis_size(axis)
        forward = [(i, (i + 1) % count) for i in range(count)]
        backward = [(target, source) for source, target in forward]
        low = lax.ppermute(lax.slice_in_dim(block, block.shape[dim] - width, None, axis=dim), axis, forward)
        high = lax.ppermute(lax.slice_in_dim(block, 0, width, axis=dim), axis, backward)
        block = jnp.concatenate([low, block, high], axis=dim)
    return block


def body(coeffs, halo_rows, edge_source, edge_target, edge_count, block_count, wigner, w_zero, w_one, w_two, attn_vector):
    width = coeffs.shape[4]
    wide = coeffs[0, 0, 0].astype(F32)
    normed = (wide * lax.rsqrt(jnp.mean(wide * wide, axis=-1, keepdims=True) + EPS)).astype(BF16)
    boundary = normed[halo_rows[0, 0, 0]]
    received = with_halo(boundary[None, None, None], (("gx", 0), ("gy", 1), ("gz", 2)), 1)
    table = jnp.concatenate([normed, received.reshape(-1, width)], axis=0)
    out = v1_call(table, edge_source[0, 0, 0], edge_target[0, 0, 0], edge_count[0, 0, 0], block_count[0, 0],
                  wigner[0, 0, 0], w_zero, w_one, w_two, attn_vector)
    return out.reshape(1, 1, 1, 128, width)


def solution(mesh):
    placed = (P("gx", "gy", "gz", None, None), P("gx", "gy", "gz", None), P("gx", "gy", "gz", None, None), P("gx", "gy", "gz", None, None),
              P("gx", "gy", "gz", None), P("gx", "gy", "gz"), P("gx", "gy", "gz", None, None, None), P(), P(), P(), P())
    return jax.shard_map(body, mesh=mesh, in_specs=placed, out_specs=P("gx", "gy", "gz", None, None), check_vma=False)
```

time: 189 us -> 116 us (0.61)
  local copies, waits for them, and re-layouts: 57.5 us -> 1.39 us
  matrix products: 36.6 us -> 0 us
  Pallas kernels: 0 us -> 30.9 us
  other arithmetic: 24.2 us -> 7.64 us
  waiting for transfers between devices: 54.9 us -> 60.8 us
    dot_general x21 -> x0, matrix products: 36.6 us -> none  [the longest x18 26.5 us: product(): return jnp.dot(left, right, preferred_element_type=jnp.float32)]
    pallas_call x0 -> x1, Pallas kernels: none -> 30.9 us  [v1_call(): pl.pallas_call(v1_kernel, out_shape=jax.ShapeDtypeStruct((128, 3200), BF1...]
    gather x3 -> x0, local copies, waits for them, and re-layouts: 16.7 us -> none  [the longest x1 10.9 us: body(): source_table[sources.reshape(-1)].reshape(home_blocks, block_size, 25, CH)]
    concatenate x3 -> x0, local copies, waits for them, and re-layouts: 12.8 us -> none  [the longest x2 12.7 us: degree_mix(): jnp.concatenate([zero_out, one_plus, one_minus, two_plus, two_minus], axi...]
    mul x5 -> x0, local copies, waits for them, and re-layouts: 11.5 us -> none  [the longest x2 9.86 us: edge_work(): mixed_one[:, CH:].reshape(edge_total, 18, CH)]
    reshape x1 -> x0, local copies, waits for them, and re-layouts: 6.72 us -> none  [body(): source_table[sources.reshape(-1)].reshape(home_blocks, block_size, 25, CH)]
    convert_element_type x3 -> x1, other arithmetic: 7.61 us -> 1.35 us  [body(): (wide * lax.rsqrt(jnp.mean(wide * wide, axis=-1, keepdims=True) + EPS)).a...]
    ppermute x3, waiting for transfers between devices: 48.9 us -> 54.8 us  [with_halo(): lax.ppermute(lax.slice_in_dim(block, block.shape[dim] - width, None, axis...]
  transfers between devices with their start and end apart: 6 -> 6, of which waited for: 5 -> 5; matrix products, arithmetic and copies ran while one was open for 4% -> 1% of each run, Pallas kernels for 0% -> 0%
where the time goes in v1:
time: 116 us
  waiting for transfers between devices  60.8 us (52%)
  Pallas kernels  30.9 us (27%)
  starting transfers between devices  14.8 us (13%)
  other arithmetic  7.64 us (7%)
  local copies, waits for them, and re-layouts  1.39 us (1%)
    ppermute x3, waiting for transfers between devices, with_halo(): lax.ppermute(lax.slice_in_dim(block, block.shape[dim] - width, None, axis...  54.8 us
    pallas_call x1, Pallas kernels, v1_call(): pl.pallas_call(v1_kernel, out_shape=jax.ShapeDtypeStruct((128, 3200), BF1...  30.9 us
    ppermute x3, starting transfers between devices, with_halo(): lax.ppermute(lax.slice_in_dim(block, block.shape[dim] - width, None, axis...  8.06 us
    ppermute x3, starting transfers between devices, with_halo(): lax.ppermute(lax.slice_in_dim(block, 0, width, axis=dim), axis, backward)  6.75 us
    ppermute x3, waiting for transfers between devices, with_halo(): lax.ppermute(lax.slice_in_dim(block, 0, width, axis=dim), axis, backward)  6.05 us
    concatenate x1, other arithmetic, body(): table = jnp.concatenate([normed, received.reshape(-1, width)], axis=0)  3.11 us
  transfers between devices with their start and end apart: 6, of which 5 were waited for; matrix products, arithmetic and copies ran while one was open for 1% of the time, Pallas kernels for 0%

profile of v1, /device:TPU:1, one launch (start us, length us, event | category | flops | bytes accessed | tf_op | source)
XLA Modules:
  0.0 116.3 jit_solution(9215160914659495204)
XLA Ops:
  0.0 0.0 copy-start
  0.0 1.4 %fusion = f32[128]{0:T(128)S(1)} fusion(bf16[1,1,1,128,3200]{4,3,2,1,0:T(8,128)(2,1)} %param.11), kind=kLoop, calls=%fused_computation.6 | loop fusion | flops 1228672 | bytes 819712 | tf_op jit(solution)/shard_map/reduce_sum | solution.py:217
  1.4 1.4 %fusion.1 = bf16[128,3200]{1,0:T(8,128)(2,1)S(1)} fusion(bf16[1,1,1,128,3200]{4,3,2,1,0:T(8,128)(2,1)} %param.11, f32[128]{0:T(128)S(1)} %add_rsqrt_fusion), kind=kLoop, calls=%fused_computation.7 | loop fusion | flops 1228800 | bytes 1638912 | tf_op jit(solution)/shard_map/convert_element_type | solution.py:217
  2.8 0.7 fusion.2
  3.5 0.7 gather_fusion
  4.2 3.6 %collective-permute-start = (bf16[1,1,1,32,3200]{4,3,2,1,0:T(8,128)(2,1)S(1)}, bf16[1,1,1,32,3200]{4,3,2,1,0:T(8,128)(2,1)S(1)}, u32[]{:S(2)}, u32[]{:S(2)}) collective-permute-start(bf16[1,1,1,32,3200]{4,3,2,1,0:T(8,128)(2,1)S(1)} %bitcast.21), channel_id=1, source_target_pairs={{0,32},{32,64},{64,96},{96,128},{128,160},{160,192},{192,224},{224... | collective-permute-start | bytes 614408 | tf_op jit(solution)/shard_map/ppermute | solution.py:208
  7.8 2.5 %collective-permute-start.1 = (bf16[1,1,1,32,3200]{4,3,2,1,0:T(8,128)(2,1)S(1)}, bf16[1,1,1,32,3200]{4,3,2,1,0:T(8,128)(2,1)S(1)}, u32[]{:S(2)}, u32[]{:S(2)}) collective-permute-start(bf16[1,1,1,32,3200]{4,3,2,1,0:T(8,128)(2,1)S(1)} %bitcast.22), channel_id=1, source_target_pairs={{32,0},{64,32},{96,64},{128,96},{160,128},{192,160},{224,192},{0,2... | collective-permute-start | bytes 614408 | tf_op jit(solution)/shard_map/ppermute | solution.py:209
  10.3 3.1 %collective-permute-done = bf16[1,1,1,32,3200]{4,3,2,1,0:T(8,128)(2,1)S(1)} collective-permute-done((bf16[1,1,1,32,3200]{4,3,2,1,0:T(8,128)(2,1)S(1)}, bf16[1,1,1,32,3200]{4,3,2,1,0:T(8,128)(2,1)S(1)}, u32[]{:S(2)}, u32[]{:S(2)}) %collective-permute-start) | collective-permute-done | bytes 204832 | tf_op jit(solution)/shard_map/ppermute | solution.py:208
  13.4 4.5 %collective-permute-done.1 = bf16[1,1,1,32,3200]{4,3,2,1,0:T(8,128)(2,1)S(1)} collective-permute-done((bf16[1,1,1,32,3200]{4,3,2,1,0:T(8,128)(2,1)S(1)}, bf16[1,1,1,32,3200]{4,3,2,1,0:T(8,128)(2,1)S(1)}, u32[]{:S(2)}, u32[]{:S(2)}) %collective-permute-start.1) | collective-permute-done | bytes 204832 | tf_op jit(solution)/shard_map/ppermute | solution.py:209
  17.9 0.1 pad_maximum_fusion.3
  18.0 2.7 %collective-permute-start.2 = (bf16[3,1,1,32,3200]{4,3,2,1,0:T(8,128)(2,1)S(1)}, bf16[3,1,1,32,3200]{4,3,2,1,0:T(8,128)(2,1)S(1)}, u32[]{:S(2)}, u32[]{:S(2)}) collective-permute-start(bf16[3,1,1,32,3200]{4,3,2,1,0:T(8,128)(2,1)S(1)} %pad_maximum_fusion.3), channel_id=1, source_target_pairs={{0,8},{8,16},{16,24},{24,0},{1,9},{9,17},{17,25},{25,1},{2,10},{10... | collective-permute-start | bytes 1843208 | tf_op jit(solution)/shard_map/ppermute | solution.py:208
  20.7 0.0 collective-permute-start.3
  20.7 12.8 %collective-permute-done.2 = bf16[3,1,1,32,3200]{4,3,2,1,0:T(8,128)(2,1)S(1)} collective-permute-done((bf16[3,1,1,32,3200]{4,3,2,1,0:T(8,128)(2,1)S(1)}, bf16[3,1,1,32,3200]{4,3,2,1,0:T(8,128)(2,1)S(1)}, u32[]{:S(2)}, u32[]{:S(2)}) %collective-permute-start.2) | collective-permute-done | bytes 614432 | tf_op jit(solution)/shard_map/ppermute | solution.py:208
  33.6 1.5 %collective-permute-done.3 = bf16[3,1,1,32,3200]{4,3,2,1,0:T(8,128)(2,1)S(1)} collective-permute-done((bf16[3,1,1,32,3200]{4,3,2,1,0:T(8,128)(2,1)S(1)}, bf16[3,1,1,32,3200]{4,3,2,1,0:T(8,128)(2,1)S(1)}, u32[]{:S(2)}, u32[]{:S(2)}) %collective-permute-start.3) | collective-permute-done | bytes 614432 | tf_op jit(solution)/shard_map/ppermute | solution.py:209
  35.1 0.3 pad_maximum_fusion.2
  35.3 1.7 %collective-permute-start.4 = (bf16[3,3,1,32,3200]{4,3,2,1,0:T(8,128)(2,1)S(1)}, bf16[3,3,1,32,3200]{4,3,2,1,0:T(8,128)(2,1)S(1)}, u32[]{:S(2)}, u32[]{:S(2)}) collective-permute-start(bf16[3,3,1,32,3200]{4,3,2,1,0:T(8,128)(2,1)S(1)} %pad_maximum_fusion.2), channel_id=1, source_target_pairs={{0,1},{1,2},{2,3},{3,4},{4,5},{5,6},{6,7},{7,0},{8,9},{9,10},{10,1... | collective-permute-start | bytes 5529608 | tf_op jit(solution)/shard_map/ppermute | solution.py:208
  37.1 4.2 %collective-permute-start.5 = (bf16[3,3,1,32,3200]{4,3,2,1,0:T(8,128)(2,1)S(1)}, bf16[3,3,1,32,3200]{4,3,2,1,0:T(8,128)(2,1)S(1)}, u32[]{:S(2)}, u32[]{:S(2)}) collective-permute-start(bf16[3,3,1,32,3200]{4,3,2,1,0:T(8,128)(2,1)S(1)} %pad_maximum_fusion.2), channel_id=1, source_target_pairs={{1,0},{2,1},{3,2},{4,3},{5,4},{6,5},{7,6},{0,7},{9,8},{10,9},{11,1... | collective-permute-start | bytes 5529608 | tf_op jit(solution)/shard_map/ppermute | solution.py:209
  41.3 0.0 copy-done
  41.3 0.7 copy.14
  42.6 38.9 %collective-permute-done.4 = bf16[3,3,1,32,3200]{4,3,2,1,0:T(8,128)(2,1)S(1)} collective-permute-done((bf16[3,3,1,32,3200]{4,3,2,1,0:T(8,128)(2,1)S(1)}, bf16[3,3,1,32,3200]{4,3,2,1,0:T(8,128)(2,1)S(1)}, u32[]{:S(2)}, u32[]{:S(2)}) %collective-permute-start.4) | collective-permute-done | bytes 1843232 | tf_op jit(solution)/shard_map/ppermute | solution.py:208
  81.5 0.0 collective-permute-done.5
  81.5 0.7 pad_maximum_fusion.1
  82.2 3.1 %pad_maximum_fusion.tab = bf16[992,3200]{1,0:T(8,128)(2,1)} fusion(bf16[864,3200]{1,0:T(8,128)(2,1)S(1)} %bitcast.20, bf16[128,3200]{1,0:T(8,128)(2,1)S(1)} %fusion.1), kind=kLoop, calls=%fused_computation.1 | loop fusion | flops 12697600 | bytes 12697600 | tf_op jit(solution)/shard_map/concatenate | solution.py:220
  85.4 30.9 %shard_map.109 = bf16[128,3200]{1,0:T(8,128)(2,1)} custom-call(s32[4]{0:T(128)} %bitcast.29, s32[1]{0:T(128)} %bitcast.19.blocks, bf16[992,3200]{1,0:T(8,128)(2,1)} %pad_maximum_fusion.tab, s32[4,128]{1,0:T(4,128)} %bitcast.27, s32[4,128]{1,0:T(4,128)} %bitcast.28, bf16[4,165,128]{2,1,0:T(8,128)(2,1)} %bitcast.26, bf16[2,640,640]{2,1,0:T(8,128)(2,1)} %wz.1, ...), custom_call_target="tpu_custom_call" | custom-call | tf_op jit(solution)/shard_map/pallas_call | solution.py:190
  (2 shorter events, 0.0 us)
Async XLA Ops:
  0.0 41.3 %copy-start = (bf16[1,1,1,4,165,128]{5,3,4,2,1,0:T(4,128)(2,1)S(1)}, bf16[1,1,1,4,165,128]{5,3,4,2,1,0:T(4,128)(2,1)}, u32[]{:S(2)}) copy-start(bf16[1,1,1,4,165,128]{5,3,4,2,1,0:T(4,128)(2,1)} %param.17) | copy-start | bytes 506884
  4.2 9.2 %collective-permute-start = (bf16[1,1,1,32,3200]{4,3,2,1,0:T(8,128)(2,1)S(1)}, bf16[1,1,1,32,3200]{4,3,2,1,0:T(8,128)(2,1)S(1)}, u32[]{:S(2)}, u32[]{:S(2)}) collective-permute-start(bf16[1,1,1,32,3200]{4,3,2,1,0:T(8,128)(2,1)S(1)} %bitcast.21), channel_id=1, source_target_pairs={{0,32},{32,64},{64,96},{96,128},{128,160},{160,192},{192,224},{224... | collective-permute-start | bytes 614408 | tf_op jit(solution)/shard_map/ppermute | solution.py:208
  7.8 10.1 %collective-permute-start.1 = (bf16[1,1,1,32,3200]{4,3,2,1,0:T(8,128)(2,1)S(1)}, bf16[1,1,1,32,3200]{4,3,2,1,0:T(8,128)(2,1)S(1)}, u32[]{:S(2)}, u32[]{:S(2)}) collective-permute-start(bf16[1,1,1,32,3200]{4,3,2,1,0:T(8,128)(2,1)S(1)} %bitcast.22), channel_id=1, source_target_pairs={{32,0},{64,32},{96,64},{128,96},{160,128},{192,160},{224,192},{0,2... | collective-permute-start | bytes 614408 | tf_op jit(solution)/shard_map/ppermute | solution.py:209
  18.0 15.5 %collective-permute-start.2 = (bf16[3,1,1,32,3200]{4,3,2,1,0:T(8,128)(2,1)S(1)}, bf16[3,1,1,32,3200]{4,3,2,1,0:T(8,128)(2,1)S(1)}, u32[]{:S(2)}, u32[]{:S(2)}) collective-permute-start(bf16[3,1,1,32,3200]{4,3,2,1,0:T(8,128)(2,1)S(1)} %pad_maximum_fusion.3), channel_id=1, source_target_pairs={{0,8},{8,16},{16,24},{24,0},{1,9},{9,17},{17,25},{25,1},{2,10},{10... | collective-permute-start | bytes 1843208 | tf_op jit(solution)/shard_map/ppermute | solution.py:208
  20.7 14.4 %collective-permute-start.3 = (bf16[3,1,1,32,3200]{4,3,2,1,0:T(8,128)(2,1)S(1)}, bf16[3,1,1,32,3200]{4,3,2,1,0:T(8,128)(2,1)S(1)}, u32[]{:S(2)}, u32[]{:S(2)}) collective-permute-start(bf16[3,1,1,32,3200]{4,3,2,1,0:T(8,128)(2,1)S(1)} %pad_maximum_fusion.3), channel_id=1, source_target_pairs={{8,0},{16,8},{24,16},{0,24},{9,1},{17,9},{25,17},{1,25},{10,2},{18... | collective-permute-start | bytes 1843208 | tf_op jit(solution)/shard_map/ppermute | solution.py:209
  35.3 46.2 %collective-permute-start.4 = (bf16[3,3,1,32,3200]{4,3,2,1,0:T(8,128)(2,1)S(1)}, bf16[3,3,1,32,3200]{4,3,2,1,0:T(8,128)(2,1)S(1)}, u32[]{:S(2)}, u32[]{:S(2)}) collective-permute-start(bf16[3,3,1,32,3200]{4,3,2,1,0:T(8,128)(2,1)S(1)} %pad_maximum_fusion.2), channel_id=1, source_target_pairs={{0,1},{1,2},{2,3},{3,4},{4,5},{5,6},{6,7},{7,0},{8,9},{9,10},{10,1... | collective-permute-start | bytes 5529608 | tf_op jit(solution)/shard_map/ppermute | solution.py:208
  37.1 44.4 %collective-permute-start.5 = (bf16[3,3,1,32,3200]{4,3,2,1,0:T(8,128)(2,1)S(1)}, bf16[3,3,1,32,3200]{4,3,2,1,0:T(8,128)(2,1)S(1)}, u32[]{:S(2)}, u32[]{:S(2)}) collective-permute-start(bf16[3,3,1,32,3200]{4,3,2,1,0:T(8,128)(2,1)S(1)} %pad_maximum_fusion.2), channel_id=1, source_target_pairs={{1,0},{2,1},{3,2},{4,3},{5,4},{6,5},{7,6},{0,7},{9,8},{10,9},{11,1... | collective-permute-start | bytes 5529608 | tf_op jit(solution)/shard_map/ppermute | solution.py:209

commit v2 on v1

v2 whole, which is shorter than its diff:
```python
import math
import functools
import jax, jax.numpy as jnp, numpy as np
from jax import lax
from jax.experimental import pallas as pl
from jax.experimental.pallas import tpu as pltpu
from jax.sharding import PartitionSpec as P

CH = 128
F32 = jnp.float32
BF16 = jnp.bfloat16
STARTS = [0, 1, 10, 35, 84]
ORDER = [0, 2, 6, 12, 20, 3, 7, 13, 21, 1, 5, 11, 19, 8, 14, 22, 4, 10, 18]
ROWS = []
for l in range(5):
    rows = []
    for pos, comp in enumerate(ORDER):
        if math.isqrt(comp) == l:
            off = comp - l * l
            rows.append((pos, [STARTS[l] + off * (2 * l + 1) + j for j in range(2 * l + 1)]))
    ROWS.append(rows)
USED = sorted({p for rows in ROWS for _, ps in rows for p in ps})
SLOT = {p: i for i, p in enumerate(USED)}
NE = 512


def rotate_out(l, wei, wb, msg):
    d = 2 * l + 1
    def step(it, _):
        e = pl.multiple_of((it % 4) * 128, 128)
        c = pl.multiple_of((it // 4) * 16, 16)
        w = [wei[pl.ds(pos * CH + c, 16), pl.ds(e, 128)].astype(F32) for pos, _ in ROWS[l]]
        for j in range(d):
            halves = []
            for h in range(2):
                acc = None
                for n, (pos, ps) in enumerate(ROWS[l]):
                    t = wb[SLOT[ps[j]], :, pl.ds(e, 128)] * w[n][8 * h:8 * h + 8]
                    acc = t if acc is None else acc + t
                halves.append(acc)
            msg[pl.ds(j * CH + c, 16), pl.ds(e, 128)] = jnp.concatenate(halves, axis=0).astype(BF16)
        return 0
    lax.fori_loop(0, 32, step, 0)


def dot(a, b):
    return jnp.dot(a, b, preferred_element_type=F32)


def conv_parts(v, x, wzt, w1t, w2t, emit):
    emit(0, 1, dot(wzt[v, 0:128, :], x[0:640, :]))
    emit(1, 2, dot(wzt[v, 128:384, :], x[0:640, :]))
    emit(3, 2, dot(wzt[v, 384:640, :], x[0:640, :]))
    for b in range(4):
        emit(5 + 2 * b, 2, dot(w1t[v, b * 256:(b + 1) * 256, :], x[640:1664, :]))
    for b in range(3):
        emit(13 + 2 * b, 2, dot(w2t[v, b * 256:(b + 1) * 256, :], x[1664:2432, :]))


P_S, P_O, P_YO, P_L, P_R, P_YC = range(6)
LINKS = ("right", "left", "yt", "zp", "zm", "partner")
CHUNKS = ((16, 5, "B"), (21, 4, "A"), (9, 4, "B"), (13, 3, "A"), (0, 5, "B"), (5, 4, "A"))
GROUPS = (((0, 1), (4,)), ((2, 3), (3,)), ((4, 5), (2, 1, 0)))


def geometry(gx, gy, gz, div, rem):
    y, xh, xl, c = div(gx, 2), rem(gx, 2), div(gy, 2), rem(gy, 2)
    xor = lambda a, b: a + b - 2 * a * b
    dev = dict(
        right=(y * 2 + xor(xh, xl), 2 * (1 - xl) + c, gz),
        left=(y * 2 + xor(xh, 1 - xl), 2 * (1 - xl) + c, gz),
        yt=(rem(y + 5 - 2 * xh, 4) * 2 + xh, gy, gz),
        ys=(rem(y + 3 + 2 * xh, 4) * 2 + xh, gy, gz),
        zp=(gx, gy, rem(gz + 1, 8)),
        zm=(gx, gy, rem(gz + 7, 8)),
        partner=(gx, 2 * xl + 1 - c, gz),
    )
    dev["relay"] = tuple(a * (1 - c) + b * c for a, b in zip(dev["right"], dev["left"]))
    s, t = 1 - 2 * xh, 1 - 2 * c
    blocks = []
    for q in range(27):
        if q < 9:
            da, db = (0, s, -s)[q // 3], 0
        else:
            p = (q - 9) // 3
            da = (0, s, -s, (1 - xl) * s, xl * s, -s)[p]
            db = (t, t, t, -t, -t, -t)[p]
        blocks.append((da + 1) * 9 + (db + 1) * 3 + q % 3)
    return dev, c, xl, blocks


def chunk_ops(k, route):
    ops = []
    S, O, YO, L, R, YC = (3 * p for p in range(6))
    dks = (1, 0, 2) if route == "A" else (1,)
    if route == "A":
        ops.append((k, "zp", S + 1, S + 0, ()))
        ops.append((k, "zm", S + 1, S + 2, ()))
    for d in dks:
        pre = () if d == 1 else ((k, S + d),)
        ops.append((k, "right", S + d, L + d, pre))
        ops.append((k, "left", S + d, R + d, pre))
    for d in dks:
        ops.append((k, "relay", "F%d" % d, O + d, ((k, L + d), (k, R + d))))
    for d in dks:
        ops.append((k, "yt", "C%d" % d, YC + d, ((k, L + d), (k, R + d))))
        ops.append((k, "yt", O + d, YO + d, ((k, O + d),)))
    if route == "B":
        for p in range(6):
            pre = () if p == 0 else ((k, 3 * p + 1),)
            ops.append((k, "zp", 3 * p + 1, 3 * p + 0, pre))
            ops.append((k, "zm", 3 * p + 1, 3 * p + 2, pre))
    for p in range(6):
        pre = tuple((k, 3 * p + d) for d in range(3) if not (p == 0 and d == 1))
        ops.append((k, "partner", 3 * p, 100 + 3 * p, pre))
    return ops


def plan(pieces, lat=1.9, rate=46.6e3):
    ops = [op for k, (_, _, r) in enumerate(CHUNKS) for op in chunk_ops(k, r)]
    pend, free, arrive, seq, now = list(ops), {}, {}, [], 0.0
    pieces = list(pieces)

    def group_ready(g):
        if g < 0:
            return 0.0
        keys = [(k, 100 + 3 * p) for k in GROUPS[g][0] for p in range(6)]
        return max(arrive.get(key, 1e9) for key in keys)

    while pend or pieces:
        ready = [op for op in pend if all(arrive.get(x, 1e9) <= now for x in op[4])]
        if ready:
            op = ready[0]
            pend.remove(op)
            seq.append(("op", op))
            k, link, _, dst, _ = op
            size = 32 * CHUNKS[k][1] * 256 * (3 if link == "partner" else 1)
            lk = "right" if link == "relay" else link
            r = 300e3 if link == "partner" else rate * (1.33 if lk == "right" else 1.0)
            start = max(now, free.get(lk, 0.0))
            free[lk] = start + size / r
            arrive[(k, dst)] = free[lk] + (1.0 if link == "partner" else lat)
            now += 0.02
            continue
        if pieces and group_ready(pieces[0][2]) <= now:
            name, us, _ = pieces.pop(0)
            seq.append(("piece", name))
            now += us
            continue
        times = [max([arrive.get(x, 1e9) for x in op[4]]) for op in pend]
        if pieces:
            times.append(group_ready(pieces[0][2]))
        now = max(now, min(times))
    return seq, now, arrive

EPS = 1e-06
NK = len(CHUNKS)


def make_pieces():
    pieces = [("own", 1.0, -1), ("onehot", 0.5, -1)]
    pieces += [("frames%d" % g, 0.35, -1) for g in range(4)]
    pieces += [("weights%d" % i, 0.35, -1) for i in range(10)]
    for gi, (_, degrees) in enumerate(GROUPS):
        lo, hi = degrees[-1] ** 2, (degrees[0] + 1) ** 2
        step = 3 if gi == len(GROUPS) - 1 else 1
        j = lo
        while j < hi:
            n = min(step, hi - j)
            pieces.append(("gather%d:%d:%d:%d" % (gi, j, n, lo), 0.28 * n, gi))
            j += n
        for l in degrees:
            for e in range(4):
                pieces.append(("rotate%d:%d:%d" % (l, e, lo), 0.01 + 0.016 * (2 * l + 1) * min(5, 2 * l + 1) / 2, gi))
    return pieces


def rotate_tile(l, e, base, gl, wb, rot):
    d = 2 * l + 1
    e0 = e * 128

    def step(it, _):
        c = pl.multiple_of(it * 16, 16)
        outs = [[] for _ in ROWS[l]]
        for h in range(2):
            g = [gl[pl.ds((base + j) * CH + c + 8 * h, 8), e0:e0 + 128] for j in range(d)]
            for n, (pos, ps) in enumerate(ROWS[l]):
                acc = None
                for j in range(d):
                    t = wb[SLOT[ps[j]], :, e0:e0 + 128] * g[j]
                    acc = t if acc is None else acc + t
                outs[n].append(acc)
        for n, (pos, ps) in enumerate(ROWS[l]):
            rot[pl.ds(pos * CH + c, 16), e0:e0 + 128] = jnp.concatenate(outs[n], axis=0).astype(BF16)
        return 0

    lax.fori_loop(0, 8, step, 0)


def weight_blocks():
    todo = []
    for v in range(2):
        todo += [(v, 0, a, b) for a in range(5) for b in range(5)]
        todo += [(v, 1, a, b) for a in range(4) for b in range(4)]
        todo += [(v, 2, a, b) for a in range(3) for b in range(3)]
    return todo


def build_block(v, m, a, b, raw, built):
    src, dst, n = raw[m], built[m], (5, 4, 3)[m]
    ra, rb = slice(a * CH, (a + 1) * CH), slice(b * CH, (b + 1) * CH)
    if m == 0:
        dst[v, rb, ra] = src[v, ra, rb].T
        return
    hb, ha = slice((n + b) * CH, (n + b + 1) * CH), slice((n + a) * CH, (n + a + 1) * CH)
    re, im = src[v, 0, ra, rb].T, src[v, 1, ra, rb].T
    dst[v, rb, ra] = re
    dst[v, hb, ha] = re
    dst[v, rb, ha] = -im
    dst[v, hb, ra] = im


def merged_kernel(cnt, blocks, src4, tgt4, halo, attn, coeffs, wig_h, wz_h, w1_h, w2_h, out,
                  cf, wig, wzr, w1r, w2r, tab, tabo, tabt, wb, wzt, w1t, w2t,
                  oh, gl, rot, act, wei, msg, attb, sigs, lsem, ssem, rsem):
    MESH = pl.DeviceIdType.MESH
    gx, gy, gz = (lax.axis_index(n) for n in ("gx", "gy", "gz"))
    dev, core, xl, bids = geometry(gx, gy, gz, lax.div, lax.rem)
    src, tgt = src4.at[0, 0, 0], tgt4.at[0, 0, 0]

    loads = [pltpu.make_async_copy(a, b, lsem.at[i]) for i, (a, b) in enumerate(
        ((coeffs.at[0, 0, 0], cf), (wig_h.at[0, 0, 0], wig), (wz_h, wzr), (w1_h, w1r), (w2_h, w2r)))]
    for cp in loads:
        cp.start()
    barrier = pltpu.get_barrier_semaphore()
    near = ("right", "left", "yt", "ys", "zp", "zm", "partner")
    for n in near:
        pl.semaphore_signal(barrier, inc=1, device_id=dev[n], device_id_type=MESH)

    pick = jnp.where(lax.broadcasted_iota(jnp.int32, (128, 32), 0) == halo[0, 0], 1.0, 0.0).astype(F32).T.astype(BF16)
    loads[0].wait()
    rows = dot(pick, cf[...])
    rows = rows * lax.rsqrt(jnp.mean(rows * rows, axis=-1, keepdims=True) + EPS)
    tab[32:64, :] = rows.astype(BF16)
    tab[864:896, :] = jnp.zeros((32, 3200), BF16)
    pl.semaphore_wait(barrier, len(near))

    descs = {}

    def issue(op):
        k, link, s, d, _ = op
        j0, n, _ = CHUNKS[k]
        cols = pl.ds(j0 * CH, n * CH)
        cnt_slots = 3 if link == "partner" else 1
        if isinstance(s, str):
            sel = core if s[0] == "F" else xl
            row = pl.multiple_of((3 * sel + int(s[1])) * 32, 32)
            sref = tabo.at[pl.ds(row, 32), cols]
        elif s < 9:
            sref = tab.at[pl.ds(32 * s, 32 * cnt_slots), cols]
        else:
            sref = tabo.at[pl.ds(32 * (s - 9), 32 * cnt_slots), cols]
        if d >= 100:
            dref = tab.at[pl.ds(288 + 32 * (d - 100), 96), cols]
        elif d < 9:
            dref = tab.at[pl.ds(32 * d, 32), cols]
        else:
            dref = tabo.at[pl.ds(32 * (d - 9), 32), cols]
        i = len(descs)
        cp = pltpu.make_async_remote_copy(src_ref=sref, dst_ref=dref, send_sem=ssem.at[i], recv_sem=rsem.at[i],
                                          device_id=dev[link], device_id_type=MESH)
        descs[(k, d)] = cp
        return cp

    waited = set()

    def arrive(key):
        if key not in waited:
            waited.add(key)
            descs[key].wait_recv()

    raw, built = (wzr, w1r, w2r), (wzt, w1t, w2t)
    wblocks = weight_blocks()

    def piece(name):
        if name == "own":
            x = cf[...].astype(F32)
            f = lax.rsqrt(jnp.mean(x * x, axis=-1, keepdims=True) + EPS)
            for j in range(25):
                tabt[j * CH:(j + 1) * CH, 0:128] = (cf[:, j * CH:(j + 1) * CH].astype(F32) * f).astype(BF16).T
        elif name == "onehot":
            own = lax.broadcasted_iota(jnp.int32, (128, 128), 0)
            for g in range(4):
                oh[0:128, g * 128:(g + 1) * 128] = jnp.where(own == src[g:g + 1, :], 1.0, 0.0).astype(BF16)
                for q in range(27):
                    at = lax.broadcasted_iota(jnp.int32, (32, 128), 0) + (128 + 32 * bids[q])
                    oh[128 + 32 * q:160 + 32 * q, g * 128:(g + 1) * 128] = jnp.where(at == src[g:g + 1, :], 1.0, 0.0).astype(BF16)
                oh[992:1024, g * 128:(g + 1) * 128] = jnp.zeros((32, 128), BF16)
        elif name.startswith("frames"):
            g = int(name[6:])
            if g == 0:
                loads[1].wait()
            for i, p in enumerate(USED):
                wb[i, :, g * 128:(g + 1) * 128] = jnp.broadcast_to(wig[g, p:p + 1, :].astype(F32), (8, 128))
        elif name.startswith("weights"):
            i = int(name[7:])
            if i == 0:
                for cp in loads[2:]:
                    cp.wait()
            for blk in wblocks[i * 10:(i + 1) * 10]:
                build_block(*blk, raw, built)
        elif name.startswith("gather"):
            gi, j0, n, lo = (int(v) for v in name[6:].split(":"))
            for j in range(j0, j0 + n):
                for g in range(7):
                    tabt[j * CH:(j + 1) * CH, 128 + g * 128:256 + g * 128] = tab[g * 128:(g + 1) * 128, j * CH:(j + 1) * CH].T
            gl[(j0 - lo) * CH:(j0 - lo + n) * CH, :] = dot(tabt[j0 * CH:(j0 + n) * CH, :], oh[...])
        elif name.startswith("rotate"):
            l, e, lo = (int(v) for v in name[6:].split(":"))
            rotate_tile(l, e, l * l - lo, gl, wb, rot)

    got = set()
    seq, _, _ = plan(make_pieces())
    for kind, what in seq:
        if kind == "op":
            for key in what[4]:
                arrive(key)
            issue(what).start()
        else:
            if what[:6] == "gather":
                g = int(what[6:].split(":")[0])
                if g not in got:
                    got.add(g)
                    for k in GROUPS[g][0]:
                        for p in range(6):
                            arrive((k, 100 + 3 * p))
            piece(what)
    for key, cp in descs.items():
        arrive(key)
        cp.wait_send()

    finish(tgt, cnt, blocks, attn, wb, wzt, w1t, w2t, out, rot, act, wei, msg, attb, sigs)


def finish(tgt, cnt, blocks, attn_ref, wb, wzt, w1t, w2t, out, rot, act, wei, msg, attb, sigs):
    attn = jnp.broadcast_to(attn_ref[...], (128, 128)).T

    def emit1(c0, n, val):
        if c0 == 0:
            sig = jax.nn.sigmoid(val)
            sigs[...] = sig
            silu = val * sig
            act[0:128, :] = silu.astype(BF16)
            for g in range(4):
                t = (silu[:, g * 128:(g + 1) * 128] * attn).reshape(8, 16, 128)
                logit = jnp.sum(t, axis=1)
                edge = lax.broadcasted_iota(jnp.int32, (8, 128), 1)
                live = jnp.logical_and(edge < cnt[0, 0, 0, g], g < blocks[0, 0, 0])
                a = jnp.where(live, jax.nn.sigmoid(logit), 0.0)
                attb[:, g * 128:(g + 1) * 128] = jnp.broadcast_to(a[:, None, :], (8, 16, 128)).reshape(128, 128)
        else:
            for k in range(n):
                act[(c0 + k) * CH:(c0 + k + 1) * CH, :] = (val[k * CH:(k + 1) * CH] * sigs[...]).astype(BF16)
    conv_parts(0, rot, wzt, w1t, w2t, emit1)

    def emit2(c0, n, val):
        for k in range(n):
            wei[(c0 + k) * CH:(c0 + k + 1) * CH, :] = (val[k * CH:(k + 1) * CH] * attb[...]).astype(BF16)
    conv_parts(1, act, wzt, w1t, w2t, emit2)

    ot = []
    for g in range(4):
        atom = lax.broadcasted_iota(jnp.int32, (128, 128), 0)
        ot.append(jnp.where(atom == tgt[g:g + 1, :], 1.0, 0.0).astype(BF16))
    ot = jnp.concatenate(ot, axis=1)
    for l in range(5):
        d = 2 * l + 1
        rotate_out(l, wei, wb, msg)
        upd = lax.dot_general(ot, msg[0:d * CH, :], (((1,), (1,)), ((), ())), preferred_element_type=F32)
        out[0, 0, 0, :, l * l * CH:(l + 1) * (l + 1) * CH] = upd.astype(BF16)


def body(coeffs, halo_rows, edge_source, edge_target, edge_count, block_count, wigner, w_zero, w_one, w_two, attn_vector):
    vm = pl.BlockSpec(memory_space=pltpu.VMEM)
    sm = pl.BlockSpec(memory_space=pltpu.SMEM)
    hb = pl.BlockSpec(memory_space=pl.ANY)
    nops = sum(len(chunk_ops(k, r)) for k, (_, _, r) in enumerate(CHUNKS))
    V = pltpu.VMEM
    return pl.pallas_call(
        merged_kernel,
        out_shape=jax.ShapeDtypeStruct((1, 1, 1, 128, 3200), BF16),
        in_specs=[sm, sm, vm, vm, vm, vm, hb, hb, hb, hb, hb],
        out_specs=vm,
        scratch_shapes=[
            V((128, 3200), BF16), V((4, 165, 128), BF16), V((2, 640, 640), BF16), V((2, 2, 512, 512), BF16), V((2, 2, 384, 384), BF16),
            V((896, 3200), BF16), V((288, 3200), BF16), V((3200, 1024), BF16), V((115, 8, NE), F32),
            V((2, 640, 640), BF16), V((2, 1024, 1024), BF16), V((2, 768, 768), BF16),
            V((1024, NE), BF16), V((9 * CH, NE), F32), V((19 * CH, NE), BF16), V((19 * CH, NE), BF16), V((19 * CH, NE), BF16),
            V((9 * CH, NE), BF16), V((CH, NE), F32), V((CH, NE), F32),
            pltpu.SemaphoreType.DMA((5,)), pltpu.SemaphoreType.DMA((nops,)), pltpu.SemaphoreType.DMA((nops,)),
        ],
        compiler_params=pltpu.CompilerParams(vmem_limit_bytes=67043328, collective_id=0, has_side_effects=True),
    )(edge_count, block_count, edge_source, edge_target, halo_rows, attn_vector.reshape(1, 128), coeffs, wigner, w_zero, w_one, w_two)


def solution(mesh):
    placed = (P("gx", "gy", "gz", None, None), P("gx", "gy", "gz", None), P("gx", "gy", "gz", None, None), P("gx", "gy", "gz", None, None),
              P("gx", "gy", "gz", None), P("gx", "gy", "gz"), P("gx", "gy", "gz", None, None, None), P(), P(), P(), P())
    return jax.shard_map(body, mesh=mesh, in_specs=placed, out_specs=P("gx", "gy", "gz", None, None), check_vma=False)
```

time: 116 us -> 61.4 us (0.53)
  waiting for transfers between devices: 60.8 us -> 0 us
  Pallas kernels: 30.9 us -> 56.9 us
  starting transfers between devices: 14.8 us -> 0 us
  other arithmetic: 7.64 us -> 0 us
  local copies, waits for them, and re-layouts: 1.39 us -> 3.7 us
    ppermute x6 -> x0, waiting for transfers between devices: 60.8 us -> none  [the longest x3 54.8 us: with_halo(): lax.ppermute(lax.slice_in_dim(block, block.shape[dim] - width, None, axis...]
    pallas_call x1, Pallas kernels: 30.9 us -> 56.9 us  [body(): pl.pallas_call(merged_kernel, out_shape=jax.ShapeDtypeStruct((1, 1, 1, 12...]
    ppermute x6 -> x0, starting transfers between devices: 14.8 us -> none  [the longest x3 8.06 us: with_halo(): lax.ppermute(lax.slice_in_dim(block, block.shape[dim] - width, None, axis...]
    concatenate x4 -> x0, other arithmetic: 4.19 us -> none  [the longest x1 3.11 us: body(): table = jnp.concatenate([normed, received.reshape(-1, width)], axis=0)]
    unnamed x3 -> x2, local copies, waits for them, and re-layouts: 0.7 us -> 3.7 us
    reduce_sum x1 -> x0, other arithmetic: 1.43 us -> none  [body(): jnp.mean(wide * wide, axis=-1, keepdims=True) + EPS]
    convert_element_type x1 -> x0, other arithmetic: 1.35 us -> none  [body(): (wide * lax.rsqrt(jnp.mean(wide * wide, axis=-1, keepdims=True) + EPS)).a...]
  transfers between devices with their start and end apart: 6 -> 0, of which waited for: 5 -> 0; matrix products, arithmetic and copies ran while one was open for 1% -> 0% of each run, Pallas kernels for 0% -> 0%
where the time goes in v2:
time: 61.4 us; the launch traced here: 61.2 us
  Pallas kernels  56.9 us (93%)
  local copies, waits for them, and re-layouts  3.7 us (6%)
  between operations  0.66 us (1%)
    pallas_call x1, Pallas kernels, body(): pl.pallas_call(merged_kernel, out_shape=jax.ShapeDtypeStruct((1, 1, 1, 12...  56.9 us
    unnamed x2, local copies, waits for them, and re-layouts  3.7 us

profile of v2, /device:TPU:1, one launch (start us, length us, event | category | flops | bytes accessed | tf_op | source)
XLA Modules:
  0.0 61.2 jit_solution(9818542780499886522)
XLA Ops:
  0.7 1.6 %copy.12.wig_h = bf16[1,1,1,4,165,128]{5,4,3,2,1,0:T(8,128)(2,1)} copy(bf16[1,1,1,4,165,128]{5,3,4,2,1,0:T(4,128)(2,1)} %param.17) | data formatting | bytes 337920 | tf_op args[6]
  2.3 56.9 %shard_map.109 = bf16[1,1,1,128,3200]{4,3,2,1,0:T(8,128)(2,1)} custom-call(s32[1,1,1,4]{3,2,1,0:T(1,128)} %cnt.1, s32[1,1,1]{2,1,0:T(1,128)S(6)} %copy.14.blocks, s32[1,1,1,4,128]{4,3,2,1,0:T(4,128)} %src4.1, s32[1,1,1,4,128]{4,3,2,1,0:T(4,128)} %tgt4.1, s32[1,1,1,32]{3,2,1,0:T(1,128)} %halo.1, f32[1,128]{1,0:T(1,128)} %bitcast.1, ...), custom_call_target="tpu_custom_call" | custom-call | tf_op jit(solution)/shard_map/pallas_call | solution.py:389
  59.1 2.1 %copy.15 = bf16[1,1,1,128,3200]{4,3,2,1,0:T(8,128)(2,1)} copy(bf16[1,1,1,128,3200]{4,3,2,1,0:T(8,128)(2,1)} %shard_map.109) | data formatting | bytes 1638400

commit v3 on v2

--- a/solution.py
+++ b/solution.py
@@ -26,21 +26,18 @@
 
 def rotate_out(l, wei, wb, msg):
     d = 2 * l + 1
-    def step(it, _):
-        e = pl.multiple_of((it % 4) * 128, 128)
-        c = pl.multiple_of((it // 4) * 16, 16)
-        w = [wei[pl.ds(pos * CH + c, 16), pl.ds(e, 128)].astype(F32) for pos, _ in ROWS[l]]
-        for j in range(d):
-            halves = []
-            for h in range(2):
-                acc = None
+    for e in range(0, NE, 128):
+        for c in range(0, CH, 16):
+            w = [wei[pos * CH + c:pos * CH + c + 16, e:e + 128].astype(F32) for pos, _ in ROWS[l]]
+            for j in range(d):
+                acc = [None, None]
                 for n, (pos, ps) in enumerate(ROWS[l]):
-                    t = wb[SLOT[ps[j]], :, pl.ds(e, 128)] * w[n][8 * h:8 * h + 8]
-                    acc = t if acc is None else acc + t
-                halves.append(acc)
-            msg[pl.ds(j * CH + c, 16), pl.ds(e, 128)] = jnp.concatenate(halves, axis=0).astype(BF16)
-        return 0
-    lax.fori_loop(0, 32, step, 0)
+                    f = wb[SLOT[ps[j]], :, e:e + 128]
+                    for h in range(2):
+                        t = f * w[n][8 * h:8 * h + 8]
+                        acc[h] = t if acc[h] is None else acc[h] + t
+                r = (l * l + j) * CH + c
+                msg[r:r + 16, e:e + 128] = jnp.concatenate(acc, axis=0).astype(BF16)
 
 
 def dot(a, b):
@@ -59,8 +56,12 @@
 
 P_S, P_O, P_YO, P_L, P_R, P_YC = range(6)
 LINKS = ("right", "left", "yt", "zp", "zm", "partner")
-CHUNKS = ((16, 5, "B"), (21, 4, "A"), (9, 4, "B"), (13, 3, "A"), (0, 5, "B"), (5, 4, "A"))
-GROUPS = (((0, 1), (4,)), ((2, 3), (3,)), ((4, 5), (2, 1, 0)))
+CHUNKS = ((16, 5, "B"), (21, 4, "A"), (9, 4, "B"), (13, 3, "A"), (4, 3, "B"), (7, 2, "A"), (0, 2, "B"), (2, 2, "A"))
+GROUPS = (((0, 1), (4,)), ((2, 3), (3,)), ((4, 5), (2,)), ((6, 7), (1, 0)))
+RPOS = (15, 16, 0, 1, 2, 17, 3, 4, 5, 18, 6, 7, 8, 9, 10, 11, 12, 13, 14)
+KZ = (3, 4, 0, 1, 2)
+KP = (6, 0, 1, 2)
+KN = (7, 3, 4, 5)
 
 
 def geometry(gx, gy, gz, div, rem):
@@ -116,7 +117,7 @@
     return ops
 
 
-def plan(pieces, lat=1.9, rate=46.6e3):
+def plan(pieces, lat=2.7, rate=46.6e3):
     ops = [op for k, (_, _, r) in enumerate(CHUNKS) for op in chunk_ops(k, r)]
     pend, free, arrive, seq, now = list(ops), {}, {}, [], 0.0
     pieces = list(pieces)
@@ -158,43 +159,40 @@
 
 
 def make_pieces():
-    pieces = [("own", 1.0, -1), ("onehot", 0.5, -1)]
-    pieces += [("frames%d" % g, 0.35, -1) for g in range(4)]
-    pieces += [("weights%d" % i, 0.35, -1) for i in range(10)]
+    pieces = [("own", 0.7, -1), ("onehot", 0.4, -1)]
+    pieces += [("frames%d" % g, 0.15, -1) for g in range(4)]
+    pieces += [("weights%d" % i, 0.3, -1) for i in range(10)]
     for gi, (_, degrees) in enumerate(GROUPS):
         lo, hi = degrees[-1] ** 2, (degrees[0] + 1) ** 2
-        step = 3 if gi == len(GROUPS) - 1 else 1
+        last = gi == len(GROUPS) - 1
+        step = hi - lo if last else 2
+        if last:
+            pieces += [("early%d" % i, 0.3, -1) for i in range(8)]
         j = lo
         while j < hi:
             n = min(step, hi - j)
-            pieces.append(("gather%d:%d:%d:%d" % (gi, j, n, lo), 0.28 * n, gi))
+            pieces.append(("gather%d:%d:%d:%d" % (gi, j, n, lo), 0.22 * n, gi))
             j += n
         for l in degrees:
             for e in range(4):
-                pieces.append(("rotate%d:%d:%d" % (l, e, lo), 0.01 + 0.016 * (2 * l + 1) * min(5, 2 * l + 1) / 2, gi))
+                pieces.append(("rotate%d:%d:%d" % (l, e, lo), 0.005 * (2 * l + 1) * min(5, 2 * l + 1), gi))
     return pieces
 
 
 def rotate_tile(l, e, base, gl, wb, rot):
     d = 2 * l + 1
     e0 = e * 128
-
-    def step(it, _):
-        c = pl.multiple_of(it * 16, 16)
-        outs = [[] for _ in ROWS[l]]
-        for h in range(2):
-            g = [gl[pl.ds((base + j) * CH + c + 8 * h, 8), e0:e0 + 128] for j in range(d)]
-            for n, (pos, ps) in enumerate(ROWS[l]):
-                acc = None
-                for j in range(d):
-                    t = wb[SLOT[ps[j]], :, e0:e0 + 128] * g[j]
-                    acc = t if acc is None else acc + t
-                outs[n].append(acc)
-        for n, (pos, ps) in enumerate(ROWS[l]):
-            rot[pl.ds(pos * CH + c, 16), e0:e0 + 128] = jnp.concatenate(outs[n], axis=0).astype(BF16)
-        return 0
-
-    lax.fori_loop(0, 8, step, 0)
+    for c in range(0, CH, 16):
+        g = [[gl[(base + j) * CH + c + 8 * h:(base + j) * CH + c + 8 * h + 8, e0:e0 + 128] for h in range(2)] for j in range(d)]
+        for pos, ps in ROWS[l]:
+            acc = [None, None]
+            for j in range(d):
+                f = wb[SLOT[ps[j]], :, e0:e0 + 128]
+                for h in range(2):
+                    t = f * g[j][h]
+                    acc[h] = t if acc[h] is None else acc[h] + t
+            r = RPOS[pos] * CH + c
+            rot[r:r + 16, e0:e0 + 128] = jnp.concatenate(acc, axis=0).astype(BF16)
 
 
 def weight_blocks():
@@ -208,28 +206,39 @@
 
 def build_block(v, m, a, b, raw, built):
     src, dst, n = raw[m], built[m], (5, 4, 3)[m]
-    ra, rb = slice(a * CH, (a + 1) * CH), slice(b * CH, (b + 1) * CH)
+    blk = lambda i: slice(i * CH, (i + 1) * CH)
     if m == 0:
-        dst[v, rb, ra] = src[v, ra, rb].T
+        dst[v, blk(b), blk(a if v else KZ[a])] = src[v, blk(a), blk(b)].T
         return
-    hb, ha = slice((n + b) * CH, (n + b + 1) * CH), slice((n + a) * CH, (n + a + 1) * CH)
-    re, im = src[v, 0, ra, rb].T, src[v, 1, ra, rb].T
-    dst[v, rb, ra] = re
-    dst[v, hb, ha] = re
-    dst[v, rb, ha] = -im
-    dst[v, hb, ra] = im
-
-
-def merged_kernel(cnt, blocks, src4, tgt4, halo, attn, coeffs, wig_h, wz_h, w1_h, w2_h, out,
-                  cf, wig, wzr, w1r, w2r, tab, tabo, tabt, wb, wzt, w1t, w2t,
-                  oh, gl, rot, act, wei, msg, attb, sigs, lsem, ssem, rsem):
+    p, q = (KP[a], KN[a]) if m == 1 and v == 0 else (a, n + a)
+    re, im = src[v, 0, blk(a), blk(b)].T, src[v, 1, blk(a), blk(b)].T
+    dst[v, blk(b), blk(p)] = re
+    dst[v, blk(n + b), blk(q)] = re
+    dst[v, blk(b), blk(q)] = -im
+    dst[v, blk(n + b), blk(p)] = im
+
+
+def early_conv(i, rot, wzt, w1t, w2t, hid):
+    if i == 0:
+        hid[0:640, :] = dot(wzt[0, :, 0:384], rot[0:384, :])
+    elif i < 5:
+        b = i - 1
+        hid[640 + b * 256:896 + b * 256, :] = dot(w1t[0, b * 256:(b + 1) * 256, 0:768], rot[384:1152, :])
+    else:
+        b = i - 5
+        hid[1664 + b * 256:1920 + b * 256, :] = dot(w2t[0, b * 256:(b + 1) * 256, :], rot[1152:1920, :])
+
+
+def merged_kernel(cnt, blocks, src_h, tgt_h, halo_h, attn_h, coeffs, wig_h, wz_h, w1_h, w2_h, out,
+                  src, tgt, halo, attn, cf, wig, wzr, w1r, w2r, tab, tabo, tabt, wb, wzt, w1t, w2t,
+                  oh, gl, rot, act, wei, msg, attb, sigs, hid, lsem, ssem, rsem):
     MESH = pl.DeviceIdType.MESH
     gx, gy, gz = (lax.axis_index(n) for n in ("gx", "gy", "gz"))
     dev, core, xl, bids = geometry(gx, gy, gz, lax.div, lax.rem)
-    src, tgt = src4.at[0, 0, 0], tgt4.at[0, 0, 0]
 
     loads = [pltpu.make_async_copy(a, b, lsem.at[i]) for i, (a, b) in enumerate(
-        ((coeffs.at[0, 0, 0], cf), (wig_h.at[0, 0, 0], wig), (wz_h, wzr), (w1_h, w1r), (w2_h, w2r)))]
+        ((halo_h.at[0, 0], halo), (coeffs.at[0, 0, 0], cf), (src_h.at[0, 0, 0], src), (tgt_h.at[0, 0, 0], tgt), (attn_h, attn),
+         (wig_h.at[0, 0, 0], wig), (wz_h, wzr), (w1_h, w1r), (w2_h, w2r)))]
     for cp in loads:
         cp.start()
     barrier = pltpu.get_barrier_semaphore()
@@ -237,8 +246,9 @@
     for n in near:
         pl.semaphore_signal(barrier, inc=1, device_id=dev[n], device_id_type=MESH)
 
-    pick = jnp.where(lax.broadcasted_iota(jnp.int32, (128, 32), 0) == halo[0, 0], 1.0, 0.0).astype(F32).T.astype(BF16)
     loads[0].wait()
+    pick = jnp.where(lax.broadcasted_iota(jnp.int32, (128, 32), 0) == halo[...], 1.0, 0.0).astype(F32).T.astype(BF16)
+    loads[1].wait()
     rows = dot(pick, cf[...])
     rows = rows * lax.rsqrt(jnp.mean(rows * rows, axis=-1, keepdims=True) + EPS)
     tab[32:64, :] = rows.astype(BF16)
@@ -289,6 +299,8 @@
             for j in range(25):
                 tabt[j * CH:(j + 1) * CH, 0:128] = (cf[:, j * CH:(j + 1) * CH].astype(F32) * f).astype(BF16).T
         elif name == "onehot":
+            for cp in loads[2:5]:
+                cp.wait()
             own = lax.broadcasted_iota(jnp.int32, (128, 128), 0)
             for g in range(4):
                 oh[0:128, g * 128:(g + 1) * 128] = jnp.where(own == src[g:g + 1, :], 1.0, 0.0).astype(BF16)
@@ -299,13 +311,13 @@
         elif name.startswith("frames"):
             g = int(name[6:])
             if g == 0:
-                loads[1].wait()
+                loads[5].wait()
             for i, p in enumerate(USED):
-                wb[i, :, g * 128:(g + 1) * 128] = jnp.broadcast_to(wig[g, p:p + 1, :].astype(F32), (8, 128))
+                wb[i, :, g * 128:(g + 1) * 128] = jnp.broadcast_to(wig[p, g:g + 1, :].astype(F32), (8, 128))
         elif name.startswith("weights"):
             i = int(name[7:])
             if i == 0:
-                for cp in loads[2:]:
+                for cp in loads[6:]:
                     cp.wait()
             for blk in wblocks[i * 10:(i + 1) * 10]:
                 build_block(*blk, raw, built)
@@ -318,6 +330,8 @@
         elif name.startswith("rotate"):
             l, e, lo = (int(v) for v in name[6:].split(":"))
             rotate_tile(l, e, l * l - lo, gl, wb, rot)
+        elif name.startswith("early"):
+            early_conv(int(name[5:]), rot, wzt, w1t, w2t, hid)
 
     got = set()
     seq, _, _ = plan(make_pieces())
@@ -339,10 +353,10 @@
         arrive(key)
         cp.wait_send()
 
-    finish(tgt, cnt, blocks, attn, wb, wzt, w1t, w2t, out, rot, act, wei, msg, attb, sigs)
-
-
-def finish(tgt, cnt, blocks, attn_ref, wb, wzt, w1t, w2t, out, rot, act, wei, msg, attb, sigs):
+    finish(tgt, cnt, blocks, attn, wb, wzt, w1t, w2t, out, oh, rot, act, wei, msg, attb, sigs, hid)
+
+
+def finish(tgt, cnt, blocks, attn_ref, wb, wzt, w1t, w2t, out, oh, rot, act, wei, msg, attb, sigs, hid):
     attn = jnp.broadcast_to(attn_ref[...], (128, 128)).T
 
     def emit1(c0, n, val):
@@ -361,23 +375,28 @@
         else:
             for k in range(n):
                 act[(c0 + k) * CH:(c0 + k + 1) * CH, :] = (val[k * CH:(k + 1) * CH] * sigs[...]).astype(BF16)
-    conv_parts(0, rot, wzt, w1t, w2t, emit1)
+    z = rot[15 * CH:17 * CH, :]
+    for c0, n in ((0, 1), (1, 2), (3, 2)):
+        emit1(c0, n, hid[c0 * CH:(c0 + n) * CH, :] + dot(wzt[0, c0 * CH:(c0 + n) * CH, 384:640], z))
+    one = rot[17 * CH:19 * CH, :]
+    for b in range(4):
+        emit1(5 + 2 * b, 2, hid[640 + b * 256:896 + b * 256, :] + dot(w1t[0, b * 256:(b + 1) * 256, 768:1024], one))
+    for b in range(3):
+        emit1(13 + 2 * b, 2, hid[1664 + b * 256:1920 + b * 256, :])
 
     def emit2(c0, n, val):
         for k in range(n):
             wei[(c0 + k) * CH:(c0 + k + 1) * CH, :] = (val[k * CH:(k + 1) * CH] * attb[...]).astype(BF16)
     conv_parts(1, act, wzt, w1t, w2t, emit2)
 
-    ot = []
     for g in range(4):
         atom = lax.broadcasted_iota(jnp.int32, (128, 128), 0)
-        ot.append(jnp.where(atom == tgt[g:g + 1, :], 1.0, 0.0).astype(BF16))
-    ot = jnp.concatenate(ot, axis=1)
+        oh[0:128, g * 128:(g + 1) * 128] = jnp.where(atom == tgt[g:g + 1, :], 1.0, 0.0).astype(BF16)
     for l in range(5):
-        d = 2 * l + 1
         rotate_out(l, wei, wb, msg)
-        upd = lax.dot_general(ot, msg[0:d * CH, :], (((1,), (1,)), ((), ())), preferred_element_type=F32)
-        out[0, 0, 0, :, l * l * CH:(l + 1) * (l + 1) * CH] = upd.astype(BF16)
+        lo, hi = l * l * CH, (l + 1) * (l + 1) * CH
+        upd = lax.dot_general(oh[0:128, :], msg[lo:hi, :], (((1,), (1,)), ((), ())), preferred_element_type=F32)
+        out[0, 0, 0, :, lo:hi] = upd.astype(BF16)
 
 
 def body(coeffs, halo_rows, edge_source, edge_target, edge_count, block_count, wigner, w_zero, w_one, w_two, attn_vector):
@@ -389,18 +408,18 @@
     return pl.pallas_call(
         merged_kernel,
         out_shape=jax.ShapeDtypeStruct((1, 1, 1, 128, 3200), BF16),
-        in_specs=[sm, sm, vm, vm, vm, vm, hb, hb, hb, hb, hb],
+        in_specs=[sm, sm] + [hb] * 9,
         out_specs=vm,
         scratch_shapes=[
-            V((128, 3200), BF16), V((4, 165, 128), BF16), V((2, 640, 640), BF16), V((2, 2, 512, 512), BF16), V((2, 2, 384, 384), BF16),
+            V((4, 128), jnp.int32), V((4, 128), jnp.int32), V((1, 32), jnp.int32), V((1, 128), F32), V((128, 3200), BF16), V((165, 4, 128), BF16), V((2, 640, 640), BF16), V((2, 2, 512, 512), BF16), V((2, 2, 384, 384), BF16),
             V((896, 3200), BF16), V((288, 3200), BF16), V((3200, 1024), BF16), V((115, 8, NE), F32),
             V((2, 640, 640), BF16), V((2, 1024, 1024), BF16), V((2, 768, 768), BF16),
             V((1024, NE), BF16), V((9 * CH, NE), F32), V((19 * CH, NE), BF16), V((19 * CH, NE), BF16), V((19 * CH, NE), BF16),
-            V((9 * CH, NE), BF16), V((CH, NE), F32), V((CH, NE), F32),
-            pltpu.SemaphoreType.DMA((5,)), pltpu.SemaphoreType.DMA((nops,)), pltpu.SemaphoreType.DMA((nops,)),
+            V((25 * CH, NE), BF16), V((CH, NE), F32), V((CH, NE), F32), V((19 * CH, NE), F32),
+            pltpu.SemaphoreType.DMA((9,)), pltpu.SemaphoreType.DMA((nops,)), pltpu.SemaphoreType.DMA((nops,)),
         ],
         compiler_params=pltpu.CompilerParams(vmem_limit_bytes=67043328, collective_id=0, has_side_effects=True),
-    )(edge_count, block_count, edge_source, edge_target, halo_rows, attn_vector.reshape(1, 128), coeffs, wigner, w_zero, w_one, w_two)
+    )(edge_count, block_count, edge_source, edge_target, halo_rows, attn_vector.reshape(1, 128), coeffs, jnp.transpose(wigner, (0, 1, 2, 4, 3, 5)), w_zero, w_one, w_two)
 
 
 def solution(mesh):

time: 61.4 us -> 54.5 us (0.89)
  Pallas kernels: 56.9 us -> 51.6 us
  local copies, waits for them, and re-layouts: 3.7 us -> 2.09 us
    pallas_call x1, Pallas kernels: 56.9 us -> 51.6 us  [body(): pl.pallas_call(merged_kernel, out_shape=jax.ShapeDtypeStruct((1, 1, 1, 12...]
    unnamed x2 -> x1, local copies, waits for them, and re-layouts: 3.7 us -> 2.09 us
where the time goes in v3:
time: 54.5 us; the launch traced here: 54.4 us
  Pallas kernels  51.6 us (95%)
  local copies, waits for them, and re-layouts  2.09 us (4%)
  between operations  0.66 us (1%)
    pallas_call x1, Pallas kernels, body(): pl.pallas_call(merged_kernel, out_shape=jax.ShapeDtypeStruct((1, 1, 1, 12...  51.6 us
    unnamed x1, local copies, waits for them, and re-layouts  2.09 us

profile of v3, /device:TPU:1, one launch (start us, length us, event | category | flops | bytes accessed | tf_op | source)
XLA Modules:
  0.0 54.4 jit_solution(10825928150977152350)
XLA Ops:
  0.7 51.6 %shard_map.109 = bf16[1,1,1,128,3200]{4,3,2,1,0:T(8,128)(2,1)} custom-call(s32[1,1,1,4]{3,2,1,0:T(1,128)} %cnt.1, s32[1,1,1]{2,1,0:T(1,128)S(6)} %copy.13.blocks, s32[1,1,1,4,128]{4,3,2,1,0:T(4,128)} %src_h.1, s32[1,1,1,4,128]{4,3,2,1,0:T(4,128)} %tgt_h.1, s32[1,1,1,32]{3,2,1,0:T(1,128)} %halo_h.1, f32[1,128]{1,0:T(1,128)} %bitcast.3, ...), custom_call_target="tpu_custom_call" | custom-call | tf_op jit(solution)/shard_map/pallas_call | solution.py:408
  52.3 2.1 %copy.14 = bf16[1,1,1,128,3200]{4,3,2,1,0:T(8,128)(2,1)} copy(bf16[1,1,1,128,3200]{4,3,2,1,0:T(8,128)(2,1)} %shard_map.109) | data formatting | bytes 1638400

commit v4 on v3

--- a/solution.py
+++ b/solution.py
@@ -56,8 +56,8 @@
 
 P_S, P_O, P_YO, P_L, P_R, P_YC = range(6)
 LINKS = ("right", "left", "yt", "zp", "zm", "partner")
-CHUNKS = ((16, 5, "B"), (21, 4, "A"), (9, 4, "B"), (13, 3, "A"), (4, 3, "B"), (7, 2, "A"), (0, 2, "B"), (2, 2, "A"))
-GROUPS = (((0, 1), (4,)), ((2, 3), (3,)), ((4, 5), (2,)), ((6, 7), (1, 0)))
+CHUNKS = ((16, 6, 'B'), (22, 3, 'A'), (9, 3, 'B'), (12, 4, 'B'), (4, 5, 'A'), (0, 4, 'B'))
+GROUPS = (((0, 1), (4,)), ((2, 3), (3,)), ((4,), (2,)), ((5,), (1, 0)))
 RPOS = (15, 16, 0, 1, 2, 17, 3, 4, 5, 18, 6, 7, 8, 9, 10, 11, 12, 13, 14)
 KZ = (3, 4, 0, 1, 2)
 KP = (6, 0, 1, 2)
@@ -117,9 +117,11 @@
     return ops
 
 
-def plan(pieces, lat=2.7, rate=46.6e3):
+def plan(pieces, lat=2.4, rate=46.6e3, window=0.3):
     ops = [op for k, (_, _, r) in enumerate(CHUNKS) for op in chunk_ops(k, r)]
-    pend, free, arrive, seq, now = list(ops), {}, {}, [], 0.0
+    group_of = {k: g for g, (ks, _) in enumerate(GROUPS) for k in ks}
+    pend = sorted(ops, key=lambda op: group_of[op[0]])
+    free, arrive, seq, now = {}, {}, [], 0.0
     pieces = list(pieces)
 
     def group_ready(g):
@@ -128,19 +130,22 @@
         keys = [(k, 100 + 3 * p) for k in GROUPS[g][0] for p in range(6)]
         return max(arrive.get(key, 1e9) for key in keys)
 
+    def link(op):
+        return "right" if op[1] == "relay" else op[1]
+
     while pend or pieces:
-        ready = [op for op in pend if all(arrive.get(x, 1e9) <= now for x in op[4])]
+        open_at = [max([arrive.get(x, 1e9) for x in op[4]] + [free.get(link(op), 0.0) - window]) for op in pend]
+        ready = [op for op, t in zip(pend, open_at) if t <= now]
         if ready:
             op = ready[0]
             pend.remove(op)
             seq.append(("op", op))
-            k, link, _, dst, _ = op
-            size = 32 * CHUNKS[k][1] * 256 * (3 if link == "partner" else 1)
-            lk = "right" if link == "relay" else link
-            r = 300e3 if link == "partner" else rate * (1.33 if lk == "right" else 1.0)
-            start = max(now, free.get(lk, 0.0))
-            free[lk] = start + size / r
-            arrive[(k, dst)] = free[lk] + (1.0 if link == "partner" else lat)
+            k, name, _, dst, _ = op
+            size = 32 * CHUNKS[k][1] * 256 * (3 if name == "partner" else 1)
+            r = 300e3 if name == "partner" else rate * (1.33 if link(op) == "right" else 1.0)
+            start = max(now, free.get(link(op), 0.0))
+            free[link(op)] = start + size / r
+            arrive[(k, dst)] = free[link(op)] + (1.0 if name == "partner" else lat)
             now += 0.02
             continue
         if pieces and group_ready(pieces[0][2]) <= now:
@@ -148,11 +153,9 @@
             seq.append(("piece", name))
             now += us
             continue
-        times = [max([arrive.get(x, 1e9) for x in op[4]]) for op in pend]
-        if pieces:
-            times.append(group_ready(pieces[0][2]))
-        now = max(now, min(times))
+        now = max(now, min(open_at + [group_ready(p[2]) for p in pieces[:1]]))
     return seq, now, arrive
+
 
 EPS = 1e-06
 NK = len(CHUNKS)

time: 54.5 us -> 51 us (0.936)
  Pallas kernels: 51.6 us -> 48.1 us
    pallas_call x1, Pallas kernels: 51.6 us -> 48.1 us  [body(): pl.pallas_call(merged_kernel, out_shape=jax.ShapeDtypeStruct((1, 1, 1, 12...]
where the time goes in v4:
time: 51 us; the launch traced here: 50.8 us
  Pallas kernels  48.1 us (94%)
  local copies, waits for them, and re-layouts  2.09 us (4%)
  between operations  0.66 us (1%)
    pallas_call x1, Pallas kernels, body(): pl.pallas_call(merged_kernel, out_shape=jax.ShapeDtypeStruct((1, 1, 1, 12...  48.1 us
    unnamed x1, local copies, waits for them, and re-layouts  2.09 us

profile of v4, /device:TPU:1, one launch (start us, length us, event | category | flops | bytes accessed | tf_op | source)
XLA Modules:
  0.0 50.8 jit_solution(15237100879386385547)
XLA Ops:
  0.7 48.1 %shard_map.109 = bf16[1,1,1,128,3200]{4,3,2,1,0:T(8,128)(2,1)} custom-call(s32[1,1,1,4]{3,2,1,0:T(1,128)} %cnt.1, s32[1,1,1]{2,1,0:T(1,128)S(6)} %copy.13.blocks, s32[1,1,1,4,128]{4,3,2,1,0:T(4,128)} %src_h.1, s32[1,1,1,4,128]{4,3,2,1,0:T(4,128)} %tgt_h.1, s32[1,1,1,32]{3,2,1,0:T(1,128)} %halo_h.1, f32[1,128]{1,0:T(1,128)} %bitcast.3, ...), custom_call_target="tpu_custom_call" | custom-call | tf_op jit(solution)/shard_map/pallas_call | solution.py:411
  48.7 2.1 %copy.14 = bf16[1,1,1,128,3200]{4,3,2,1,0:T(8,128)(2,1)} copy(bf16[1,1,1,128,3200]{4,3,2,1,0:T(8,128)(2,1)} %shard_map.109) | data formatting | bytes 1638400

commit v5 on v4

--- a/solution.py
+++ b/solution.py
@@ -24,9 +24,9 @@
 NE = 512
 
 
-def rotate_out(l, wei, wb, msg):
+def rotate_out(l, e4, wei, wb, msg):
     d = 2 * l + 1
-    for e in range(0, NE, 128):
+    for e in (e4 * 128,):
         for c in range(0, CH, 16):
             w = [wei[pos * CH + c:pos * CH + c + 16, e:e + 128].astype(F32) for pos, _ in ROWS[l]]
             for j in range(d):
@@ -42,16 +42,6 @@
 
 def dot(a, b):
     return jnp.dot(a, b, preferred_element_type=F32)
-
-
-def conv_parts(v, x, wzt, w1t, w2t, emit):
-    emit(0, 1, dot(wzt[v, 0:128, :], x[0:640, :]))
-    emit(1, 2, dot(wzt[v, 128:384, :], x[0:640, :]))
-    emit(3, 2, dot(wzt[v, 384:640, :], x[0:640, :]))
-    for b in range(4):
-        emit(5 + 2 * b, 2, dot(w1t[v, b * 256:(b + 1) * 256, :], x[640:1664, :]))
-    for b in range(3):
-        emit(13 + 2 * b, 2, dot(w2t[v, b * 256:(b + 1) * 256, :], x[1664:2432, :]))
 
 
 P_S, P_O, P_YO, P_L, P_R, P_YC = range(6)
@@ -214,11 +204,12 @@
         dst[v, blk(b), blk(a if v else KZ[a])] = src[v, blk(a), blk(b)].T
         return
     p, q = (KP[a], KN[a]) if m == 1 and v == 0 else (a, n + a)
+    s, t = (2 * b, 2 * b + 1) if v else (b, n + b)
     re, im = src[v, 0, blk(a), blk(b)].T, src[v, 1, blk(a), blk(b)].T
-    dst[v, blk(b), blk(p)] = re
-    dst[v, blk(n + b), blk(q)] = re
-    dst[v, blk(b), blk(q)] = -im
-    dst[v, blk(n + b), blk(p)] = im
+    dst[v, blk(s), blk(p)] = re
+    dst[v, blk(t), blk(q)] = re
+    dst[v, blk(s), blk(q)] = -im
+    dst[v, blk(t), blk(p)] = im
 
 
 def early_conv(i, rot, wzt, w1t, w2t, hid):
@@ -234,7 +225,7 @@
 
 def merged_kernel(cnt, blocks, src_h, tgt_h, halo_h, attn_h, coeffs, wig_h, wz_h, w1_h, w2_h, out,
                   src, tgt, halo, attn, cf, wig, wzr, w1r, w2r, tab, tabo, tabt, wb, wzt, w1t, w2t,
-                  oh, gl, rot, act, wei, msg, attb, sigs, hid, lsem, ssem, rsem):
+                  oh, gl, rot, act, wei, msg, attb, sigs, hid, obuf, osem, lsem, ssem, rsem):
     MESH = pl.DeviceIdType.MESH
     gx, gy, gz = (lax.axis_index(n) for n in ("gx", "gy", "gz"))
     dev, core, xl, bids = geometry(gx, gy, gz, lax.div, lax.rem)
@@ -356,10 +347,10 @@
         arrive(key)
         cp.wait_send()
 
-    finish(tgt, cnt, blocks, attn, wb, wzt, w1t, w2t, out, oh, rot, act, wei, msg, attb, sigs, hid)
-
-
-def finish(tgt, cnt, blocks, attn_ref, wb, wzt, w1t, w2t, out, oh, rot, act, wei, msg, attb, sigs, hid):
+    finish(tgt, cnt, blocks, attn, wb, wzt, w1t, w2t, out, oh, rot, act, wei, msg, attb, sigs, hid, obuf, osem)
+
+
+def finish(tgt, cnt, blocks, attn_ref, wb, wzt, w1t, w2t, out, oh, rot, act, wei, msg, attb, sigs, hid, obuf, osem):
     attn = jnp.broadcast_to(attn_ref[...], (128, 128)).T
 
     def emit1(c0, n, val):
@@ -387,23 +378,46 @@
     for b in range(3):
         emit1(13 + 2 * b, 2, hid[1664 + b * 256:1920 + b * 256, :])
 
-    def emit2(c0, n, val):
-        for k in range(n):
-            wei[(c0 + k) * CH:(c0 + k + 1) * CH, :] = (val[k * CH:(k + 1) * CH] * attb[...]).astype(BF16)
-    conv_parts(1, act, wzt, w1t, w2t, emit2)
-
     for g in range(4):
         atom = lax.broadcasted_iota(jnp.int32, (128, 128), 0)
         oh[0:128, g * 128:(g + 1) * 128] = jnp.where(atom == tgt[g:g + 1, :], 1.0, 0.0).astype(BF16)
-    for l in range(5):
-        rotate_out(l, wei, wb, msg)
+
+    def mix(l, m):
+        if m == 0:
+            val = dot(wzt[1, l * CH:(l + 1) * CH, :], act[0:640, :])
+            places = (l,)
+        elif m == 1:
+            val = dot(w1t[1, (l - 1) * 256:l * 256, :], act[640:1664, :])
+            places = (4 + l, 8 + l)
+        else:
+            val = dot(w2t[1, (l - 2) * 256:(l - 1) * 256, :], act[1664:2432, :])
+            places = (11 + l, 14 + l)
+        for i, pos in enumerate(places):
+            wei[pos * CH:(pos + 1) * CH, :] = (val[i * CH:(i + 1) * CH] * attb[...]).astype(BF16)
+
+    def scatter(l):
         lo, hi = l * l * CH, (l + 1) * (l + 1) * CH
         upd = lax.dot_general(oh[0:128, :], msg[lo:hi, :], (((1,), (1,)), ((), ())), preferred_element_type=F32)
-        out[0, 0, 0, :, lo:hi] = upd.astype(BF16)
+        obuf[:, lo:hi] = upd.astype(BF16)
+        cp = pltpu.make_async_copy(obuf.at[:, pl.ds(lo, hi - lo)], out.at[0, 0, 0, :, pl.ds(lo, hi - lo)], osem.at[l])
+        cp.start()
+        return cp
+
+    for m in range(3):
+        mix(4, m)
+    writes = []
+    for l in (4, 3, 2, 1, 0):
+        todo = [(l - 1, m) for m in range(min(l, 3))] if l else []
+        for e in range(4):
+            if todo:
+                mix(*todo.pop(0))
+            rotate_out(l, e, wei, wb, msg)
+        writes.append(scatter(l))
+    for cp in writes:
+        cp.wait()
 
 
 def body(coeffs, halo_rows, edge_source, edge_target, edge_count, block_count, wigner, w_zero, w_one, w_two, attn_vector):
-    vm = pl.BlockSpec(memory_space=pltpu.VMEM)
     sm = pl.BlockSpec(memory_space=pltpu.SMEM)
     hb = pl.BlockSpec(memory_space=pl.ANY)
     nops = sum(len(chunk_ops(k, r)) for k, (_, _, r) in enumerate(CHUNKS))
@@ -412,13 +426,13 @@
         merged_kernel,
         out_shape=jax.ShapeDtypeStruct((1, 1, 1, 128, 3200), BF16),
         in_specs=[sm, sm] + [hb] * 9,
-        out_specs=vm,
+        out_specs=hb,
         scratch_shapes=[
             V((4, 128), jnp.int32), V((4, 128), jnp.int32), V((1, 32), jnp.int32), V((1, 128), F32), V((128, 3200), BF16), V((165, 4, 128), BF16), V((2, 640, 640), BF16), V((2, 2, 512, 512), BF16), V((2, 2, 384, 384), BF16),
             V((896, 3200), BF16), V((288, 3200), BF16), V((3200, 1024), BF16), V((115, 8, NE), F32),
             V((2, 640, 640), BF16), V((2, 1024, 1024), BF16), V((2, 768, 768), BF16),
             V((1024, NE), BF16), V((9 * CH, NE), F32), V((19 * CH, NE), BF16), V((19 * CH, NE), BF16), V((19 * CH, NE), BF16),
-            V((25 * CH, NE), BF16), V((CH, NE), F32), V((CH, NE), F32), V((19 * CH, NE), F32),
+            V((25 * CH, NE), BF16), V((CH, NE), F32), V((CH, NE), F32), V((19 * CH, NE), F32), V((128, 3200), BF16), pltpu.SemaphoreType.DMA((5,)),
             pltpu.SemaphoreType.DMA((9,)), pltpu.SemaphoreType.DMA((nops,)), pltpu.SemaphoreType.DMA((nops,)),
         ],
         compiler_params=pltpu.CompilerParams(vmem_limit_bytes=67043328, collective_id=0, has_side_effects=True),

time: 51 us -> 50.6 us (level)
  no operation moved by 1% of the time
where the time goes in v5:
time: 50.6 us; the launch traced here: 50.5 us
  Pallas kernels  47.7 us (94%)
  local copies, waits for them, and re-layouts  2.09 us (4%)
  between operations  0.66 us (1%)
    pallas_call x1, Pallas kernels, body(): pl.pallas_call(merged_kernel, out_shape=jax.ShapeDtypeStruct((1, 1, 1, 12...  47.7 us
    unnamed x1, local copies, waits for them, and re-layouts  2.09 us

profile of v5, /device:TPU:1, one launch (start us, length us, event | category | flops | bytes accessed | tf_op | source)
XLA Modules:
  0.0 50.5 jit_solution(12325489825897137580)
XLA Ops:
  0.7 47.7 %shard_map.109 = bf16[1,1,1,128,3200]{4,3,2,1,0:T(8,128)(2,1)} custom-call(s32[1,1,1,4]{3,2,1,0:T(1,128)} %cnt.1, s32[1,1,1]{2,1,0:T(1,128)S(6)} %copy.13.blocks, s32[1,1,1,4,128]{4,3,2,1,0:T(4,128)} %src_h.1, s32[1,1,1,4,128]{4,3,2,1,0:T(4,128)} %tgt_h.1, s32[1,1,1,32]{3,2,1,0:T(1,128)} %halo_h.1, f32[1,128]{1,0:T(1,128)} %bitcast.3, ...), custom_call_target="tpu_custom_call" | custom-call | tf_op jit(solution)/shard_map/pallas_call | solution.py:425
  48.4 2.1 %copy.14 = bf16[1,1,1,128,3200]{4,3,2,1,0:T(8,128)(2,1)} copy(bf16[1,1,1,128,3200]{4,3,2,1,0:T(8,128)(2,1)} %shard_map.109) | data formatting | bytes 1638400
